TPU v7x, 8 devices: a whole 2x2x1 slice. The times are simulated.
8 devices in a mesh: grp: 1 (over z), dz: 2 (over y), dy: 2 (over x), dx: 2 (over core).
Axes of the slice: x: 2, y: 2, z: 1, core: 2. Of those that a mesh axis runs over, the one named last changes fastest.
Arguments:
- x_in: bfloat16 [8192, 3072], P(('grp', 'dx', 'dz'), 'dy')
- w_gate: bfloat16 [3072, 8192], P('dy', ('dz', 'dx'))
- w_up: bfloat16 [3072, 8192], P('dy', ('dz', 'dx'))
- w_down: bfloat16 [8192, 3072], P('dz', ('dy', 'dx'))
Outputs:
- output: bfloat16 [8192, 3072], P(('grp', 'dx', 'dz'), 'dy')
All inputs are finite; a program needn't handle non-finite values.
Results may differ from a plain program's by a relative error of at most 0.0124721.
Values are sent between devices in bfloat16 or wider.
A program may use at most 1 GiB of HBM per device.

v0:
```python
import jax
import jax.numpy as jnp
from jax import lax
from jax.sharding import PartitionSpec as P


def solution(mesh):
    x_spec = P(("grp", "dx", "dz"), "dy")
    w_in_spec = P("dy", ("dz", "dx"))
    w_out_spec = P("dz", ("dy", "dx"))

    def local_mlp(x_blk, wg_blk, wu_blk, wd_blk):
        x_rows = lax.all_gather(x_blk, "dz", axis=0, tiled=True)
        wg_cols = lax.all_gather(wg_blk, "dx", axis=1, tiled=True)
        wu_cols = lax.all_gather(wu_blk, "dx", axis=1, tiled=True)
        gate_part = jnp.dot(x_rows, wg_cols, preferred_element_type=jnp.float32)
        up_part = jnp.dot(x_rows, wu_cols, preferred_element_type=jnp.float32)
        gate_sum = lax.psum_scatter(gate_part, "dy", scatter_dimension=0, tiled=True)
        up_sum = lax.psum_scatter(up_part, "dy", scatter_dimension=0, tiled=True)
        gate_val = gate_sum.astype(jnp.bfloat16).astype(jnp.float32)
        up_val = up_sum.astype(jnp.bfloat16).astype(jnp.float32)
        hidden = (jax.nn.silu(gate_val) * up_val).astype(jnp.bfloat16)
        h_rows = lax.all_gather(hidden, "dy", axis=0, tiled=True)
        wd_cols = lax.all_gather(wd_blk, "dx", axis=1, tiled=True)
        out_part = jnp.dot(h_rows, wd_cols, preferred_element_type=jnp.float32)
        out_sum = lax.psum_scatter(out_part, "dz", scatter_dimension=0, tiled=True)
        return out_sum.astype(jnp.bfloat16)

    return jax.shard_map(local_mlp, mesh=mesh, in_specs=(x_spec, w_in_spec, w_in_spec, w_out_spec), out_specs=x_spec, check_vma=False)
```

profile of v0, /device:TPU:0, one launch (start us, length us, event | category | flops | bytes accessed | tf_op | source)
XLA Modules:
  0.0 2470.5 jit_solution(9123670592838307311)
XLA Ops:
  6.5 0.7 all-gather.6.cloned.1.call-update
  7.3 0.0 all-gather.8.cloned.1.call-start
  7.3 0.7 all-gather.8.cloned.1.call-update
  8.0 0.0 all-gather.10.cloned.1.call-start
  8.1 0.7 all-gather.10.cloned.1.call-update
  8.7 0.0 reduce-scatter.4.cloned.1.call-start
  8.8 153.5 %all-gather.6.cloned.1.call-done = bf16[4096,1536]{1,0:T(8,128)(2,1)} async-done(((bf16[2048,1536]{1,0:T(8,128)(2,1)}), bf16[4096,1536]{1,0:T(8,128)(2,1)}) %all-gather.6.cloned.1.call-update) | async-done | bytes 12582928 | tf_op jit(solution)/shard_map/all_gather | solution.py:13
  162.3 24.4 all-gather.8.cloned.1.call-done
  186.7 61.7 %fusion.5 = f32[4096,4096]{1,0:T(8,128)} fusion(bf16[4096,1536]{1,0:T(8,128)(2,1)} %all-gather.6.cloned.1.call-done, bf16[1536,4096]{1,0:T(8,128)(2,1)} %all-gather.8.cloned.1.call-done), kind=kOutput, calls=%fused_computation.7 | convolution fusion | flops 51539607552 | bytes 92274688 | tf_op jit(solution)/shard_map/dot_general | solution.py:16
  248.5 0.2 reduce-scatter.6.cloned.1.call-start
  248.7 0.0 all-gather.10.cloned.1.call-done
  248.7 61.7 %fusion.6 = f32[4096,4096]{1,0:T(8,128)} fusion(bf16[4096,1536]{1,0:T(8,128)(2,1)} %all-gather.6.cloned.1.call-done, bf16[1536,4096]{1,0:T(8,128)(2,1)} %all-gather.10.cloned.1.call-done), kind=kOutput, calls=%fused_computation.8 | convolution fusion | flops 51539607552 | bytes 92274688 | tf_op jit(solution)/shard_map/dot_general | solution.py:17
  310.5 0.0 all-gather.14.cloned.1.call-start
  310.5 0.5 all-gather.14.cloned.1.call-update
  311.0 0.0 all-gather.12.cloned.1.call-start
  311.1 664.3 %reduce-scatter.4.cloned.1.call-done = f32[2048,4096]{1,0:T(8,128)} async-done(((f32[4096,4096]{1,0:T(8,128)}), f32[2048,4096]{1,0:T(8,128)}) %reduce-scatter.4.cloned.1.call-update) | async-done | bytes 33554448 | tf_op jit(solution)/shard_map/reduce_scatter | solution.py:18
  975.4 727.8 %reduce-scatter.6.cloned.1.call-done = f32[2048,4096]{1,0:T(8,128)} async-done(((f32[4096,4096]{1,0:T(8,128)}), f32[2048,4096]{1,0:T(8,128)}) %reduce-scatter.6.cloned.1.call-update) | async-done | bytes 33554448 | tf_op jit(solution)/shard_map/reduce_scatter | solution.py:19
  1703.2 27.5 %fusion.4 = bf16[2048,4096]{1,0:T(8,128)(2,1)} fusion(f32[2048,4096]{1,0:T(8,128)} %reduce-scatter.6.cloned.1.call-done, f32[2048,4096]{1,0:T(8,128)} %reduce-scatter.4.cloned.1.call-done), kind=kLoop, calls=%fused_computation.6 | loop fusion | flops 83886080 | bytes 83886080 | tf_op jit(solution)/shard_map/convert_element_type | solution.py:22
  1730.7 0.3 reduce-scatter.8.cloned.1.call-start
  1731.0 0.0 all-gather.14.cloned.1.call-done
  1731.0 385.4 %all-gather.12.cloned.1.call-done = bf16[4096,4096]{1,0:T(8,128)(2,1)} async-done(((bf16[2048,4096]{1,0:T(8,128)(2,1)}), bf16[4096,4096]{1,0:T(8,128)(2,1)}) %all-gather.12.cloned.1.call-update) | async-done | bytes 33554448 | tf_op jit(solution)/shard_map/all_gather | solution.py:23
  2116.4 62.5 %fusion.7 = f32[4096,1536]{1,0:T(8,128)} fusion(bf16[4096,4096]{1,0:T(8,128)(2,1)} %all-gather.12.cloned.1.call-done, bf16[4096,1536]{1,0:T(8,128)(2,1)} %all-gather.14.cloned.1.call-done), kind=kOutput, calls=%fused_computation.9 | convolution fusion | flops 51539607552 | bytes 71303168 | tf_op jit(solution)/shard_map/dot_general | solution.py:25
  2178.9 276.6 %reduce-scatter.8.cloned.1.call-done = f32[2048,1536]{1,0:T(8,128)} async-done(((f32[4096,1536]{1,0:T(8,128)}), f32[2048,1536]{1,0:T(8,128)}) %reduce-scatter.8.cloned.1.call-update) | async-done | bytes 12582928 | tf_op jit(solution)/shard_map/reduce_scatter | solution.py:26
  2455.6 8.1 convert_element_type.23
  (5 shorter events, 0.1 us)
Async XLA Ops:
  6.5 155.7 %all-gather.6.cloned.1.call-start = ((), (), s32[]{:S(2)}) async-start(), calls=%async_computation.3 | async-start | bytes 18874368 | tf_op jit(solution)/shard_map/all_gather | solution.py:13
  7.3 179.5 %all-gather.8.cloned.1.call-start = ((), (), s32[]{:S(2)}) async-start(), calls=%async_computation.4 | async-start | bytes 18874368 | tf_op jit(solution)/shard_map/all_gather | solution.py:14
  8.0 240.7 %all-gather.10.cloned.1.call-start = ((), (), s32[]{:S(2)}) async-start(), calls=%async_computation.6 | async-start | bytes 18874368 | tf_op jit(solution)/shard_map/all_gather | solution.py:15
  8.7 966.7 %reduce-scatter.4.cloned.1.call-start = ((), (), s32[]{:S(2)}) async-start(), calls=%async_computation.5 | async-start | bytes 100663296 | tf_op jit(solution)/shard_map/reduce_scatter | solution.py:18
  248.5 1454.7 %reduce-scatter.6.cloned.1.call-start = ((), (), s32[]{:S(2)}) async-start(), calls=%async_computation.7 | async-start | bytes 100663296 | tf_op jit(solution)/shard_map/reduce_scatter | solution.py:19
  310.5 1420.5 %all-gather.14.cloned.1.call-start = ((), (), s32[]{:S(2)}) async-start(), calls=%async_computation.9 | async-start | bytes 18874368 | tf_op jit(solution)/shard_map/all_gather | solution.py:24
  311.0 1805.3 %all-gather.12.cloned.1.call-start = ((), (), s32[]{:S(2)}) async-start(), calls=%async_computation.8 | async-start | bytes 50331648 | tf_op jit(solution)/shard_map/all_gather | solution.py:23
  1730.7 724.9 %reduce-scatter.8.cloned.1.call-start = ((), (), s32[]{:S(2)}) async-start(), calls=%async_computation.10 | async-start | bytes 37748736 | tf_op jit(solution)/shard_map/reduce_scatter | solution.py:26
Sparse Core Ops, SparseCore 0:
  8.9 153.3 all-gather.5
  163.8 22.8 all-gather.7
  188.2 24.0 all-gather.9
  248.6 726.7 reduce-scatter.3
  977.5 725.6 reduce-scatter.5
  1704.6 22.8 all-gather.13
  1730.8 385.4 all-gather.11
  2179.1 276.4 reduce-scatter.7
where the time goes:
time: 2470 us
  waiting for transfers between devices  2230 us (90%)
  matrix products  186 us (8%)
  other arithmetic  35.6 us (1%)
    reduce_scatter x1, waiting for transfers between devices, local_mlp(): up_sum = lax.psum_scatter(up_part, 'dy', scatter_dimension=0, tiled=True)  728 us
    reduce_scatter x1, waiting for transfers between devices, local_mlp(): lax.psum_scatter(gate_part, 'dy', scatter_dimension=0, tiled=True)  664 us
    all_gather x1, waiting for transfers between devices, local_mlp(): h_rows = lax.all_gather(hidden, 'dy', axis=0, tiled=True)  385 us
    reduce_scatter x1, waiting for transfers between devices, local_mlp(): out_sum = lax.psum_scatter(out_part, 'dz', scatter_dimension=0, tiled=True)  277 us
    all_gather x1, waiting for transfers between devices, local_mlp(): x_rows = lax.all_gather(x_blk, 'dz', axis=0, tiled=True)  153 us
    dot_general x1, matrix products, local_mlp(): out_part = jnp.dot(h_rows, wd_cols, preferred_element_type=jnp.float32)  62.5 us
    dot_general x1, matrix products, local_mlp(): gate_part = jnp.dot(x_rows, wg_cols, preferred_element_type=jnp.float32)  61.7 us
    dot_general x1, matrix products, local_mlp(): up_part = jnp.dot(x_rows, wu_cols, preferred_element_type=jnp.float32)  61.7 us
  transfers between devices with their start and end apart: 8, of which 6 were waited for; matrix products, arithmetic and copies ran while one was open for 6% of the time, Pallas kernels for 0%

commit v1 on v0

v1 whole, which is shorter than its diff:
```python
import jax
import jax.numpy as jnp
from jax import lax
from jax.experimental import pallas as pl
from jax.experimental.pallas import tpu as pltpu
from jax.sharding import PartitionSpec as P

MESH = pl.DeviceIdType.MESH
BF16 = jnp.bfloat16
F32 = jnp.float32


def make_local_mlp(x_shape, w_shape, d_shape):
    rows, dh = x_shape
    fq = w_shape[1]
    fh, dq = d_shape
    ra = rows // 2
    w = 256
    nc = fq // w
    la = 4
    cw = 256
    npr = dq // cw
    nk = 4 * npr
    xc = 2
    xrc = ra // xc
    tm = 512
    own, oth = ra, 0

    def kernel(x, wg, wu, wd,
               z, wdy, wpo, wpx, ddy, dpo, dpx, zr,
               xg, h, wbuf, dbuf, zs, zin, zo,
               xs, xr, wys, wyr, wos, wor, wfs, wfr,
               dys, dyr, dos, dor, dfs, dfr, zss, zsr, zos, zor, zls, lds):
        dz = lax.axis_index("dz")
        dy = lax.axis_index("dy")
        dx = lax.axis_index("dx")
        to_dz = {"dz": 1 - dz}
        to_dy = {"dy": 1 - dy}
        to_dx = {"dx": 1 - dx}

        def rcopy(src, dst, ss, rs, dev):
            return pltpu.make_async_remote_copy(
                src_ref=src, dst_ref=dst, send_sem=ss, recv_sem=rs, device_id=dev, device_id_type=MESH)

        mine = pl.multiple_of(dy * ra, ra)
        theirs = pl.multiple_of((1 - dy) * ra, ra)
        left, right = pl.ds(0, dh), pl.ds(dh, dh)

        def x_dy(i):
            return rcopy(x.at[pl.ds(theirs + i * xrc, xrc)], xg.at[pl.ds(own + i * xrc, xrc), right],
                         xs.at[i], xr.at[i], to_dy)

        def x_fw(i):
            return rcopy(xg.at[pl.ds(own + i * xrc, xrc), right], xg.at[pl.ds(oth + i * xrc, xrc), right],
                         xs.at[xc + i], xr.at[xc + i], to_dz)

        x_dz = rcopy(x.at[pl.ds(mine, ra)], xg.at[pl.ds(oth, ra), left], xs.at[2 * xc], xr.at[2 * xc], to_dz)
        x_lo = pltpu.make_async_copy(x.at[pl.ds(mine, ra)], xg.at[pl.ds(own, ra), left], lds.at[0])

        def cols(j):
            return pl.ds(pl.multiple_of(j * w, w), w)

        def w_dy(j):
            return [rcopy(src.at[:, cols(j)], wdy.at[j, t], wys.at[j, t], wyr.at[j, t], to_dy)
                    for t, src in enumerate((wg, wu))]

        def w_own(j):
            return [rcopy(src.at[:, cols(j)], wpo.at[j, t], wos.at[j, t], wor.at[j, t], to_dx)
                    for t, src in enumerate((wg, wu))]

        def w_fw(j):
            return [rcopy(wdy.at[j, t], wpx.at[j, t], wfs.at[j, t], wfr.at[j, t], to_dx) for t in range(2)]

        def dcols(p):
            return pl.ds(pl.multiple_of(p * cw, cw), cw)

        def d_dy(p):
            return rcopy(wd.at[:, dcols(p)], ddy.at[p], dys.at[p], dyr.at[p], to_dy)

        def d_own(p):
            return rcopy(wd.at[:, dcols(p)], dpo.at[p], dos.at[p], dor.at[p], to_dx)

        def d_fw(p):
            return rcopy(ddy.at[p], dpx.at[p], dfs.at[p], dfr.at[p], to_dx)

        def start(cs):
            for c in cs:
                c.start()

        def wait_all(cs):
            for c in cs:
                c.wait()

        def wait_recv(cs):
            for c in cs:
                c.wait_recv()

        barrier = pltpu.get_barrier_semaphore()
        for dev in (to_dx, to_dy, to_dz):
            pl.semaphore_signal(barrier, inc=1, device_id=dev, device_id_type=MESH)
        pl.semaphore_wait(barrier, 3)

        for i in range(xc):
            x_dy(i).start()
        x_dz.start()
        x_lo.start()

        @pl.loop(0, la)
        def _(j):
            start(w_dy(j))
            start(w_own(j))

        for i in range(xc):
            x_dy(i).wait_recv()
            x_fw(i).start()
        x_lo.wait()
        x_dz.wait_recv()
        for i in range(xc):
            x_fw(i).wait_recv()

        def gate_up(slot, first, last, hcol):
            @pl.loop(first, last)
            def _(r):
                rs = pl.ds(pl.multiple_of(r * tm, tm), tm)
                xt = xg[rs, :]
                g = jnp.dot(xt, wbuf[slot, 0], preferred_element_type=F32).astype(BF16).astype(F32)
                u = jnp.dot(xt, wbuf[slot, 1], preferred_element_type=F32).astype(BF16).astype(F32)
                h[rs, pl.ds(pl.multiple_of(hcol, w), w)] = (g * jax.nn.sigmoid(g) * u).astype(BF16)

        nt = 2 * ra // tm

        @pl.loop(0, nc)
        def _(j):
            @pl.when(j + la < nc)
            def _():
                start(w_dy(j + la))
                start(w_own(j + la))

            @pl.when(jnp.logical_and(j >= la, j < la + npr))
            def _():
                d_dy(j - la).start()
                d_own(j - la).start()

            wait_recv(w_dy(j))
            start(w_fw(j))
            ld0 = [pltpu.make_async_copy(wg.at[:, cols(j)], wbuf.at[0, 0, left], lds.at[0]),
                   pltpu.make_async_copy(wu.at[:, cols(j)], wbuf.at[0, 1, left], lds.at[1]),
                   pltpu.make_async_copy(wdy.at[j, 0], wbuf.at[0, 0, right], lds.at[2]),
                   pltpu.make_async_copy(wdy.at[j, 1], wbuf.at[0, 1, right], lds.at[3])]
            start(ld0)
            wait_all(ld0)
            gate_up(0, 0, nt // 2, dx * fq + j * w)
            wait_recv(w_own(j))
            wait_recv(w_fw(j))
            ld1 = [pltpu.make_async_copy(wpo.at[j, 0], wbuf.at[1, 0, left], lds.at[4]),
                   pltpu.make_async_copy(wpo.at[j, 1], wbuf.at[1, 1, left], lds.at[5]),
                   pltpu.make_async_copy(wpx.at[j, 0], wbuf.at[1, 0, right], lds.at[6]),
                   pltpu.make_async_copy(wpx.at[j, 1], wbuf.at[1, 1, right], lds.at[7])]
            start(ld1)
            gate_up(0, nt // 2, nt, dx * fq + j * w)
            wait_all(ld1)
            gate_up(1, 0, nt, (1 - dx) * fq + j * w)

        def split(k):
            return k // (2 * npr), (k % (2 * npr)) // 2, k % 2

        def load_d(k, slot):
            half, p, q = split(k)
            for hh in range(2):
                for qq in range(2):
                    @pl.when(jnp.logical_and(half == hh, q == qq))
                    def _(hh=hh, qq=qq):
                        src = ((wd.at[:, dcols(p)], dpo.at[p]), (ddy.at[p], dpx.at[p]))[hh][qq]
                        c = pltpu.make_async_copy(src, dbuf.at[slot], lds.at[slot])
                        c.start()
                        c.wait()

        def z_send(k):
            return rcopy(zs.at[k % 3], zr.at[k], zss.at[k], zsr.at[k], to_dz)

        def out_cols(m):
            _, p, q = split(m)
            return pl.ds(pl.multiple_of(((dx + q) % 2) * dq + p * cw, cw), cw)

        def out_local(m):
            return pltpu.make_async_copy(zo.at[m % 2], z.at[pl.ds(mine, ra), out_cols(m)], zls.at[m % 2])

        def out_remote(m):
            i = m - 2 * npr
            return rcopy(zo.at[m % 2], z.at[pl.ds(mine, ra), out_cols(m)], zos.at[i], zor.at[i], to_dy)

        def in_remote(m):
            i = m - 2 * npr
            return rcopy(zo.at[m % 2], z.at[pl.ds(theirs, ra), out_cols(m)], zos.at[i], zor.at[i], to_dy)

        @pl.loop(0, nk + 2)
        def _(k):
            half, p, q = split(k)

            @pl.when(k < nk)
            def _():
                @pl.when(jnp.logical_and(half == 0, q == 1))
                def _():
                    d_own(p).wait_recv()

                @pl.when(jnp.logical_and(half == 1, q == 1))
                def _():
                    d_fw(p).wait_recv()

                load_d(k, 0)

                @pl.when(k >= 3)
                def _():
                    z_send(k - 3).wait_send()

                @pl.loop(0, ra // tm)
                def _(r):
                    rs = pl.ds(pl.multiple_of(r * tm, tm), tm)
                    zs[k % 3, rs] = jnp.dot(h[pl.ds(pl.multiple_of(oth + r * tm, tm), tm), :], dbuf[0],
                                            preferred_element_type=F32)

                z_send(k).start()

            f = k - (2 * npr - 1)

            @pl.when(jnp.logical_and(f >= 0, jnp.logical_and(f < 2 * npr, f % 2 == 0)))
            def _():
                d_dy(f // 2).wait_recv()
                d_fw(f // 2).start()

            @pl.when(k >= 2)
            def _():
                m = k - 2
                load_d(m, 1)
                z_send(m).wait_recv()
                c = pltpu.make_async_copy(zr.at[m], zin, lds.at[2])
                c.start()

                @pl.when(jnp.logical_and(m >= 2, m < 2 * npr + 2))
                def _():
                    out_local(m - 2).wait()

                @pl.when(m >= 2 * npr + 2)
                def _():
                    out_remote(m - 2).wait_send()

                c.wait()

                @pl.loop(0, ra // tm)
                def _(r):
                    rs = pl.ds(pl.multiple_of(r * tm, tm), tm)
                    acc = jnp.dot(h[pl.ds(pl.multiple_of(own + r * tm, tm), tm), :], dbuf[1],
                                  preferred_element_type=F32)
                    zo[m % 2, rs] = (acc + zin[rs]).astype(BF16)

                @pl.when(m < 2 * npr)
                def _():
                    out_local(m).start()

                @pl.when(m >= 2 * npr)
                def _():
                    out_remote(m).start()

        for m in (nk - 2, nk - 1):
            out_remote(m).wait_send()
        for m in range(2 * npr, nk):
            in_remote(m).wait_recv()
        for k in range(nk - 3, nk):
            z_send(k).wait_send()
        for i in range(xc):
            x_dy(i).wait_send()
            x_fw(i).wait_send()
        x_dz.wait_send()

        @pl.loop(0, nc)
        def _(j):
            for c in w_dy(j) + w_own(j) + w_fw(j):
                c.wait_send()

        @pl.loop(0, npr)
        def _(p):
            d_dy(p).wait_send()
            d_own(p).wait_send()
            d_fw(p).wait_send()

    def sd(shape, dtype=BF16):
        return jax.ShapeDtypeStruct(shape, dtype)

    wl = sd((nc, 2, dh, w))
    dl = sd((npr, fh, cw))
    outs = (sd((rows, dh)), wl, wl, wl, dl, dl, dl, sd((nk, ra, cw), F32))
    dma = pltpu.SemaphoreType.DMA
    return pl.pallas_call(
        kernel,
        out_shape=outs,
        in_specs=[pl.BlockSpec(memory_space=pl.ANY)] * 4,
        out_specs=[pl.BlockSpec(memory_space=pl.ANY)] * len(outs),
        scratch_shapes=[
            pltpu.VMEM((rows, 2 * dh), BF16),
            pltpu.VMEM((rows, fh), BF16),
            pltpu.VMEM((2, 2, 2 * dh, w), BF16),
            pltpu.VMEM((2, fh, cw), BF16),
            pltpu.VMEM((3, ra, cw), F32),
            pltpu.VMEM((ra, cw), F32),
            pltpu.VMEM((2, ra, cw), BF16),
            dma((2 * xc + 1,)), dma((2 * xc + 1,)),
            dma((nc, 2)), dma((nc, 2)), dma((nc, 2)), dma((nc, 2)), dma((nc, 2)), dma((nc, 2)),
            dma((npr,)), dma((npr,)), dma((npr,)), dma((npr,)), dma((npr,)), dma((npr,)),
            dma((nk,)), dma((nk,)), dma((2 * npr,)), dma((2 * npr,)), dma((2,)), dma((8,)),
        ],
        compiler_params=pltpu.CompilerParams(
            collective_id=0, has_side_effects=True, vmem_limit_bytes=62 * 1024 * 1024),
    )


def solution(mesh):
    x_spec = P(("grp", "dx", "dz"), "dy")
    w_in_spec = P("dy", ("dz", "dx"))
    w_out_spec = P("dz", ("dy", "dx"))

    def local_mlp(x_blk, wg_blk, wu_blk, wd_blk):
        return make_local_mlp(x_blk.shape, wg_blk.shape, wd_blk.shape)(x_blk, wg_blk, wu_blk, wd_blk)[0]

    return jax.shard_map(local_mlp, mesh=mesh, in_specs=(x_spec, w_in_spec, w_in_spec, w_out_spec), out_specs=x_spec, check_vma=False)
```

time: 2470 us -> 657 us (0.27)
  waiting for transfers between devices: 2230 us -> 0 us
  Pallas kernels: 0 us -> 649 us
  matrix products: 186 us -> 0 us
  other arithmetic: 35.6 us -> 0 us
    reduce_scatter x3 -> x0, waiting for transfers between devices: 1670 us -> none  [the longest x1 728 us: local_mlp(): up_sum = lax.psum_scatter(up_part, 'dy', scatter_dimension=0, tiled=True)]
    pallas_call x0 -> x1, Pallas kernels: none -> 649 us  [local_mlp(): make_local_mlp(x_blk.shape, wg_blk.shape, wd_blk.shape)]
    all_gather x5 -> x0, waiting for transfers between devices: 563 us -> none  [the longest x1 385 us: local_mlp(): h_rows = lax.all_gather(hidden, 'dy', axis=0, tiled=True)]
    dot_general x3 -> x0, matrix products: 186 us -> none  [the longest x1 62.5 us: local_mlp(): out_part = jnp.dot(h_rows, wd_cols, preferred_element_type=jnp.float32)]
    convert_element_type x2 -> x0, other arithmetic: 35.6 us -> none  [the longest x1 27.5 us: local_mlp(): hidden = (jax.nn.silu(gate_val) * up_val).astype(jnp.bfloat16)]
  transfers between devices with their start and end apart: 8 -> 0, of which waited for: 6 -> 0; matrix products, arithmetic and copies ran while one was open for 6% -> 0% of each run, Pallas kernels for 0% -> 0%
where the time goes in v1:
time: 657 us; the launch traced here: 655 us
  Pallas kernels  649 us (99%)
    pallas_call x1, Pallas kernels, local_mlp(): make_local_mlp(x_blk.shape, wg_blk.shape, wd_blk.shape)  649 us

profile of v1, /device:TPU:0, one launch (start us, length us, event | category | flops | bytes accessed | tf_op | source)
XLA Modules:
  0.0 655.2 jit_solution(12228776970232816925)
XLA Ops:
  0.0 649.3 %shard_map.46 = (bf16[2048,1536]{1,0:T(8,128)(2,1)}, bf16[8,2,1536,256]{3,2,1,0:T(8,128)(2,1)}, bf16[8,2,1536,256]{3,2,1,0:T(8,128)(2,1)}, bf16[8,2,1536,256]{3,...) custom-call(bf16[2048,1536]{1,0:T(8,128)(2,1)} %x.1, ...), custom_call_target="tpu_custom_call" | custom-call | tf_op jit(solution)/shard_map/pallas_call | solution.py:322
  649.3 5.9 copy.6

commit v2 on v1

v2 whole, which is shorter than its diff:
```python
import jax
import jax.numpy as jnp
from jax import lax
from jax.experimental import pallas as pl
from jax.experimental.pallas import tpu as pltpu
from jax.sharding import PartitionSpec as P

MESH = pl.DeviceIdType.MESH
BF16 = jnp.bfloat16
F32 = jnp.float32


def make_local_mlp(x_shape, w_shape, d_shape):
    rows, dh = x_shape
    fq = w_shape[1]
    fh, dq = d_shape
    ra = rows // 2
    w = 256
    nc = fq // w
    la = 4
    cw = 256
    npr = dq // cw
    tm = 512
    nz = ra // tm
    ne = tm
    ve = npr - 1
    xc = 2
    xrc = ra // xc
    nl = 2 * ve
    nk = nl + nz * (4 * npr - 2 * ve)
    no = nz * 2 * npr
    lag = 3
    own, oth = ra, 0

    def kernel(x, wg, wu, wd,
               z, wdy, wpo, wpx, ddy, dpo, dpx, d2o, d2p, zr,
               xg, h, h2, wbuf, dbuf, zs, zin, zacc, zo,
               xs, xr, wys, wyr, wos, wor, wfs, wfr, hs, hr,
               dys, dyr, dos, dor, dfs, dfr, d2s, d2r, d2t, d2u,
               zss, zsr, zos, zor, zls, lds):
        dz = lax.axis_index("dz")
        dy = lax.axis_index("dy")
        dx = lax.axis_index("dx")
        to_dz = {"dz": 1 - dz}
        to_dy = {"dy": 1 - dy}
        to_dx = {"dx": 1 - dx}

        def rcopy(src, dst, ss, rs, dev):
            return pltpu.make_async_remote_copy(
                src_ref=src, dst_ref=dst, send_sem=ss, recv_sem=rs, device_id=dev, device_id_type=MESH)

        mine = pl.multiple_of(dy * ra, ra)
        theirs = pl.multiple_of((1 - dy) * ra, ra)
        left, right = pl.ds(0, dh), pl.ds(dh, dh)

        def x_dy(i):
            return rcopy(x.at[pl.ds(theirs + i * xrc, xrc)], xg.at[pl.ds(own + i * xrc, xrc), right],
                         xs.at[i], xr.at[i], to_dy)

        def x_fw(i):
            return rcopy(xg.at[pl.ds(own + i * xrc, xrc), right], xg.at[pl.ds(oth + i * xrc, xrc), right],
                         xs.at[xc + i], xr.at[xc + i], to_dz)

        x_dz = rcopy(x.at[pl.ds(mine, ra)], xg.at[pl.ds(oth, ra), left], xs.at[2 * xc], xr.at[2 * xc], to_dz)
        x_lo = pltpu.make_async_copy(x.at[pl.ds(mine, ra)], xg.at[pl.ds(own, ra), left], lds.at[0])

        def cols(j):
            return pl.ds(pl.multiple_of(j * w, w), w)

        def w_dy(j):
            return [rcopy(src.at[:, cols(j)], wdy.at[j, t], wys.at[j, t], wyr.at[j, t], to_dy)
                    for t, src in enumerate((wg, wu))]

        def w_own(j):
            return [rcopy(src.at[:, cols(j)], wpo.at[j, t], wos.at[j, t], wor.at[j, t], to_dx)
                    for t, src in enumerate((wg, wu))]

        def w_fw(j):
            return [rcopy(wdy.at[j, t], wpx.at[j, t], wfs.at[j, t], wfr.at[j, t], to_dx) for t in range(2)]

        def dcols(p):
            return pl.ds(pl.multiple_of(p * cw, cw), cw)

        def d_dy(p):
            return rcopy(wd.at[:, dcols(p)], ddy.at[p], dys.at[p], dyr.at[p], to_dy)

        def d_own(p):
            return rcopy(wd.at[:, dcols(p)], dpo.at[p], dos.at[p], dor.at[p], to_dx)

        def d_fw(p):
            return rcopy(ddy.at[p], dpx.at[p], dfs.at[p], dfr.at[p], to_dx)

        def d2_dz(p):
            return rcopy(wd.at[:, dcols(p)], d2o.at[p], d2s.at[p], d2r.at[p], to_dz)

        def d2_fw(p):
            return rcopy(d2o.at[p], d2p.at[p], d2t.at[p], d2u.at[p], to_dx)

        def hcols(j, t):
            return pl.ds(pl.multiple_of(((dx + t) % 2) * fq + j * w, w), w)

        def h_dz(j, t):
            return rcopy(h.at[pl.ds(oth, ne), hcols(j, t)], h2.at[:, hcols(j, t)], hs.at[j, t], hr.at[j, t], to_dz)

        def start(cs):
            for c in cs:
                c.start()

        def wait_all(cs):
            for c in cs:
                c.wait()

        def wait_recv(cs):
            for c in cs:
                c.wait_recv()

        barrier = pltpu.get_barrier_semaphore()
        for dev in (to_dx, to_dy, to_dz):
            pl.semaphore_signal(barrier, inc=1, device_id=dev, device_id_type=MESH)
        pl.semaphore_wait(barrier, 3)

        for i in range(xc):
            x_dy(i).start()
        x_dz.start()
        x_lo.start()

        @pl.loop(0, la)
        def _(j):
            start(w_dy(j))
            start(w_own(j))

        for i in range(xc):
            x_dy(i).wait_recv()
            x_fw(i).start()
        for p in range(ve):
            d2_dz(p).start()
        x_lo.wait()
        x_dz.wait_recv()
        for i in range(xc):
            x_fw(i).wait_recv()

        def gate_up(slot, row, hc):
            rs = pl.ds(pl.multiple_of(row, tm), tm)
            xt = xg[rs, :]
            g = jnp.dot(xt, wbuf[slot, 0], preferred_element_type=F32).astype(BF16).astype(F32)
            u = jnp.dot(xt, wbuf[slot, 1], preferred_element_type=F32).astype(BF16).astype(F32)
            h[rs, hc] = (g * jax.nn.sigmoid(g) * u).astype(BF16)

        def own_rows(j):
            @pl.loop(0, 2 * nz)
            def _(i):
                t = i // nz
                gate_up(t, own + (i % nz) * tm, hcols(j, t))

        @pl.loop(0, nc)
        def _(j):
            @pl.when(j + la < nc)
            def _():
                start(w_dy(j + la))
                start(w_own(j + la))

            @pl.when(jnp.logical_and(j >= la, j < la + npr))
            def _():
                d_dy(j - la).start()
                d_own(j - la).start()

            @pl.when(jnp.logical_and(j >= la + 1, j < la + 1 + ve))
            def _():
                d2_dz(j - la - 1).wait_recv()
                d2_fw(j - la - 1).start()

            wait_recv(w_dy(j))
            start(w_fw(j))
            ld0 = [pltpu.make_async_copy(wg.at[:, cols(j)], wbuf.at[0, 0, left], lds.at[0]),
                   pltpu.make_async_copy(wu.at[:, cols(j)], wbuf.at[0, 1, left], lds.at[1]),
                   pltpu.make_async_copy(wdy.at[j, 0], wbuf.at[0, 0, right], lds.at[2]),
                   pltpu.make_async_copy(wdy.at[j, 1], wbuf.at[0, 1, right], lds.at[3])]
            start(ld0)
            wait_all(ld0)
            ld1 = [pltpu.make_async_copy(wpo.at[j, 0], wbuf.at[1, 0, left], lds.at[4]),
                   pltpu.make_async_copy(wpo.at[j, 1], wbuf.at[1, 1, left], lds.at[5]),
                   pltpu.make_async_copy(wpx.at[j, 0], wbuf.at[1, 0, right], lds.at[6]),
                   pltpu.make_async_copy(wpx.at[j, 1], wbuf.at[1, 1, right], lds.at[7])]

            @pl.loop(0, 2 * nz)
            def _(i):
                t = i // nz

                @pl.when(i == 1)
                def _():
                    wait_recv(w_own(j))
                    wait_recv(w_fw(j))
                    start(ld1)

                @pl.when(i == nz)
                def _():
                    wait_all(ld1)

                gate_up(t, oth + (i % nz) * tm, hcols(j, t))

                @pl.when(i >= nz)
                def _():
                    h_dz(j, i - nz).start()

            @pl.when(j < nc - 1)
            def _():
                own_rows(j)

        def split(k):
            late = (k + nk - nl) // nk
            s = (k - nl) // nz + nk
            first = s - nk
            lastc = 2 * npr + 1
            other = (first + lastc - 1) // lastc - first // lastc
            half = late * other
            p = (1 - late) * (k // 2) + late * (other * ((first + 2 * npr - 1) // 2 - npr) + (1 - other) * (npr - 1))
            q = (1 - late) * (k % 2) + late * (other * ((first + 1) % 2) + (1 - other) * (first // lastc))
            r = (1 - late) * (nz - 1) + late * ((k + nl) % nz)
            return half, p, q, r

        def chunk_src(half, p, q):
            return ((wd.at[:, dcols(p)], dpo.at[p]), (ddy.at[p], dpx.at[p]))[half][q]

        def load_d(k, slot):
            half, p, q, r = split(k)
            for hh in range(2):
                for qq in range(2):
                    @pl.when(jnp.logical_and(jnp.logical_or(k < nl, r == 0), jnp.logical_and(half == hh, q == qq)))
                    def _(hh=hh, qq=qq):
                        c = pltpu.make_async_copy(chunk_src(hh, p, qq), dbuf.at[slot], lds.at[slot])
                        c.start()
                        c.wait()

        def z_send(k):
            return rcopy(zs.at[k % (lag + 1)], zr.at[k], zss.at[k], zsr.at[k], to_dz)

        def out_cols(p, q):
            return pl.ds(pl.multiple_of(((dx + q) % 2) * dq + p * cw, cw), cw)

        def out_at(m, base):
            half, p, q, r = split(m)
            return z.at[pl.ds(pl.multiple_of(base + r * tm, tm), tm), out_cols(p, q)]

        def is_other(m):
            return split(m)[0] == 1

        def out_local(m):
            return pltpu.make_async_copy(zo.at[m % 2], out_at(m, mine), zls.at[m % 2])

        def out_remote(m):
            i = m - (nl + nz)
            return rcopy(zo.at[m % 2], out_at(m, mine), zos.at[i], zor.at[i], to_dy)

        def in_remote(m):
            i = m - (nl + nz)
            return rcopy(zo.at[m % 2], out_at(m, theirs), zos.at[i], zor.at[i], to_dy)

        def free_out(m):
            @pl.when(is_other(m))
            def _():
                out_remote(m).wait_send()

            @pl.when(jnp.logical_not(is_other(m)))
            def _():
                out_local(m).wait()

        def send_piece(k):
            half, p, q, r = split(k)

            @pl.when(jnp.logical_and(q == 1, jnp.logical_or(k < nl, r == 0)))
            def _():
                @pl.when(half == 0)
                def _():
                    d_own(p).wait_recv()

                @pl.when(half == 1)
                def _():
                    d_fw(p).wait_recv()

            load_d(k, 0)

            @pl.when(k > lag)
            def _():
                z_send(k - lag - 1).wait_send()

            zs[k % (lag + 1)] = jnp.dot(h[pl.ds(pl.multiple_of(oth + r * tm, tm), tm), :], dbuf[0],
                                        preferred_element_type=F32)
            z_send(k).start()

        def e_out(e):
            return pltpu.make_async_copy(zo.at[2], z.at[pl.ds(mine, ne), out_cols(e // 2, e % 2)], zls.at[2])

        def e_piece(e):
            p = e // 2
            for qq in range(2):
                @pl.when(e % 2 == qq)
                def _(qq=qq):
                    c = [pltpu.make_async_copy(chunk_src(0, p, qq), dbuf.at[2], lds.at[2]),
                         pltpu.make_async_copy((d2o, d2p)[qq].at[p], dbuf.at[3], lds.at[3])]
                    start(c)
                    wait_all(c)

            acc = jnp.dot(h[pl.ds(own, ne), :], dbuf[2], preferred_element_type=F32)
            acc = acc + jnp.dot(h2[...], dbuf[3], preferred_element_type=F32)

            @pl.when(e >= 1)
            def _():
                e_out(e - 1).wait()

            zo[2] = acc.astype(BF16)
            e_out(e).start()

        e0 = 5

        @pl.loop(0, nk + lag)
        def _(k):
            @pl.when(k < nk)
            def _():
                send_piece(k)

            @pl.when(k == lag - 1)
            def _():
                own_rows(nc - 1)

            f = k - (nl + nz - 1)

            @pl.when(jnp.logical_and(f >= 0, jnp.logical_and(f < 2 * nz * npr, f % (2 * nz) == 0)))
            def _():
                d_dy(f // (2 * nz)).wait_recv()
                d_fw(f // (2 * nz)).start()

            @pl.when(k == e0 - 1)
            def _():
                for p in range(ve):
                    d2_fw(p).wait_recv()

                @pl.loop(0, nc)
                def _(j):
                    for t in range(2):
                        h_dz(j, t).wait_recv()

            @pl.when(jnp.logical_and(k >= e0, jnp.logical_and(k < e0 + 4 * ve, (k - e0) % 2 == 0)))
            def _():
                e_piece((k - e0) // 2)

            @pl.when(k >= lag)
            def _():
                m = k - lag
                half, p, q, r = split(m)
                load_d(m, 1)
                zacc[...] = jnp.dot(h[pl.ds(pl.multiple_of(own + r * tm, tm), tm), :], dbuf[1],
                                    preferred_element_type=F32)

                @pl.when(m >= 2)
                def _():
                    free_out(m - 2)

                z_send(m).wait_recv()
                c = pltpu.make_async_copy(zr.at[m], zin, lds.at[4])
                c.start()
                c.wait()
                zo[m % 2] = (zacc[...] + zin[...]).astype(BF16)

                @pl.when(half == 0)
                def _():
                    out_local(m).start()

                @pl.when(half == 1)
                def _():
                    out_remote(m).start()

        for m in (nk - 2, nk - 1):
            out_local(m).wait()
        e_out(2 * ve - 1).wait()
        for k in range(nk - lag - 1, nk):
            z_send(k).wait_send()
        for i in range(xc):
            x_dy(i).wait_send()
            x_fw(i).wait_send()
        x_dz.wait_send()

        @pl.loop(0, nc)
        def _(j):
            for c in w_dy(j) + w_own(j) + w_fw(j) + [h_dz(j, 0), h_dz(j, 1)]:
                c.wait_send()

        @pl.loop(0, npr)
        def _(p):
            d_dy(p).wait_send()
            d_own(p).wait_send()
            d_fw(p).wait_send()

        @pl.loop(0, ve)
        def _(p):
            d2_dz(p).wait_send()
            d2_fw(p).wait_send()

        @pl.loop(nl + nz, nl + nz + no)
        def _(m):
            in_remote(m).wait_recv()

    def sd(shape, dtype=BF16):
        return jax.ShapeDtypeStruct(shape, dtype)

    wl = sd((nc, 2, dh, w))
    dl = sd((npr, fh, cw))
    el = sd((ve, fh, cw))
    outs = (sd((rows, dh)), wl, wl, wl, dl, dl, dl, el, el, sd((nk, tm, cw), F32))
    dma = pltpu.SemaphoreType.DMA
    return pl.pallas_call(
        kernel,
        out_shape=outs,
        in_specs=[pl.BlockSpec(memory_space=pl.ANY)] * 4,
        out_specs=[pl.BlockSpec(memory_space=pl.ANY)] * len(outs),
        scratch_shapes=[
            pltpu.VMEM((rows, 2 * dh), BF16),
            pltpu.VMEM((rows, fh), BF16),
            pltpu.VMEM((ne, fh), BF16),
            pltpu.VMEM((2, 2, 2 * dh, w), BF16),
            pltpu.VMEM((4, fh, cw), BF16),
            pltpu.VMEM((lag + 1, tm, cw), F32),
            pltpu.VMEM((tm, cw), F32),
            pltpu.VMEM((tm, cw), F32),
            pltpu.VMEM((3, tm, cw), BF16),
            dma((2 * xc + 1,)), dma((2 * xc + 1,)),
            dma((nc, 2)), dma((nc, 2)), dma((nc, 2)), dma((nc, 2)), dma((nc, 2)), dma((nc, 2)), dma((nc, 2)), dma((nc, 2)),
            dma((npr,)), dma((npr,)), dma((npr,)), dma((npr,)), dma((npr,)), dma((npr,)),
            dma((ve,)), dma((ve,)), dma((ve,)), dma((ve,)),
            dma((nk,)), dma((nk,)), dma((no,)), dma((no,)), dma((3,)), dma((8,)),
        ],
        compiler_params=pltpu.CompilerParams(
            collective_id=0, has_side_effects=True, vmem_limit_bytes=62 * 1024 * 1024),
    )


def solution(mesh):
    x_spec = P(("grp", "dx", "dz"), "dy")
    w_in_spec = P("dy", ("dz", "dx"))
    w_out_spec = P("dz", ("dy", "dx"))

    def local_mlp(x_blk, wg_blk, wu_blk, wd_blk):
        return make_local_mlp(x_blk.shape, wg_blk.shape, wd_blk.shape)(x_blk, wg_blk, wu_blk, wd_blk)[0]

    return jax.shard_map(local_mlp, mesh=mesh, in_specs=(x_spec, w_in_spec, w_in_spec, w_out_spec), out_specs=x_spec, check_vma=False)
```

time: 657 us -> 600 us (0.913)
  Pallas kernels: 649 us -> 592 us
    pallas_call x1, Pallas kernels: 649 us -> 592 us  [local_mlp(): make_local_mlp(x_blk.shape, wg_blk.shape, wd_blk.shape)]
where the time goes in v2:
time: 600 us; the launch traced here: 598 us
  Pallas kernels  592 us (99%)
    pallas_call x1, Pallas kernels, local_mlp(): make_local_mlp(x_blk.shape, wg_blk.shape, wd_blk.shape)  592 us

profile of v2, /device:TPU:0, one launch (start us, length us, event | category | flops | bytes accessed | tf_op | source)
XLA Modules:
  0.0 597.9 jit_solution(14769142084517390399)
XLA Ops:
  0.0 592.0 %shard_map.46 = (bf16[2048,1536]{1,0:T(8,128)(2,1)}, bf16[8,2,1536,256]{3,2,1,0:T(8,128)(2,1)}, bf16[8,2,1536,256]{3,2,1,0:T(8,128)(2,1)}, bf16[8,2,1536,256]{3,...) custom-call(bf16[2048,1536]{1,0:T(8,128)(2,1)} %x.1, ...), custom_call_target="tpu_custom_call" | custom-call | tf_op jit(solution)/shard_map/pallas_call | solution.py:442
  592.0 5.9 copy.6

commit v3 on v2

v3 whole, which is shorter than its diff:
```python
import jax
import jax.numpy as jnp
from jax import lax
from jax.experimental import pallas as pl
from jax.experimental.pallas import tpu as pltpu
from jax.sharding import PartitionSpec as P

MESH = pl.DeviceIdType.MESH
BF16 = jnp.bfloat16
F32 = jnp.float32


def make_local_mlp(x_shape, w_shape, d_shape):
    rows, dh = x_shape
    fq = w_shape[1]
    fh, dq = d_shape
    ra = rows // 2
    w = 128
    nc = fq // w
    la = 8
    cw = 256
    npr = dq // cw
    tm = 512
    nz = ra // tm
    ne = tm
    nl = 2 * npr - 1
    nk = nl + nz * (4 * npr - nl)
    no = nz * 2 * npr
    lag = 3
    xc = 2
    xrc = ra // xc
    own, oth = ra, 0

    def kernel(x, wg, wu, wd,
               z, wdy, wpo, wpx, ddy, dpo, dpx, d2o, d2p, zr,
               xg, h, h2, wbuf, dbuf, zs, zin, zacc, zo,
               xs, xr, wys, wyr, wfs, wfr, hs, hr, bs, br,
               dys, dyr, dfs, dfr, d2s, d2r, d2t, d2u,
               zss, zsr, zos, zor, zls, lds):
        dz = lax.axis_index("dz")
        dy = lax.axis_index("dy")
        dx = lax.axis_index("dx")
        to_dz = {"dz": 1 - dz}
        to_dy = {"dy": 1 - dy}
        to_dx = {"dx": 1 - dx}

        def rcopy(src, dst, ss, rs, dev):
            return pltpu.make_async_remote_copy(
                src_ref=src, dst_ref=dst, send_sem=ss, recv_sem=rs, device_id=dev, device_id_type=MESH)

        mine = pl.multiple_of(dy * ra, ra)
        theirs = pl.multiple_of((1 - dy) * ra, ra)
        left, right = pl.ds(0, dh), pl.ds(dh, dh)

        def x_dy(i):
            return rcopy(x.at[pl.ds(theirs + i * xrc, xrc)], xg.at[pl.ds(own + i * xrc, xrc), right],
                         xs.at[i], xr.at[i], to_dy)

        def x_fw(i):
            return rcopy(xg.at[pl.ds(own + i * xrc, xrc), right], xg.at[pl.ds(oth + i * xrc, xrc), right],
                         xs.at[xc + i], xr.at[xc + i], to_dz)

        x_dz = rcopy(x.at[pl.ds(mine, ra)], xg.at[pl.ds(oth, ra), left], xs.at[2 * xc], xr.at[2 * xc], to_dz)
        x_lo = pltpu.make_async_copy(x.at[pl.ds(mine, ra)], xg.at[pl.ds(own, ra), left], lds.at[8])

        def cols(j):
            return pl.ds(pl.multiple_of(j * w, w), w)

        def w_dy(j):
            return [rcopy(src.at[:, cols(j)], wdy.at[j, t], wys.at[j, t], wyr.at[j, t], to_dy)
                    for t, src in enumerate((wg, wu))]

        def w_fw(j):
            return [rcopy(wdy.at[j, t], wpx.at[j, t], wfs.at[j, t], wfr.at[j, t], to_dx) for t in range(2)]

        def dcols(p):
            return pl.ds(pl.multiple_of(p * cw, cw), cw)

        def d_dy(p):
            return rcopy(wd.at[:, dcols(p)], ddy.at[p], dys.at[p], dyr.at[p], to_dy)

        def d_fw(p):
            return rcopy(ddy.at[p], dpx.at[p], dfs.at[p], dfr.at[p], to_dx)

        bulk = [rcopy(src, dst, bs.at[i], br.at[i], to_dx)
                for i, (src, dst) in enumerate(((wg, wpo.at[0]), (wu, wpo.at[1]), (wd, dpo)))]

        def d2_dz(p):
            return rcopy(wd.at[:, dcols(p)], d2o.at[p], d2s.at[p], d2r.at[p], to_dz)

        def d2_fw(p):
            return rcopy(d2o.at[p], d2p.at[p], d2t.at[p], d2u.at[p], to_dx)

        def hcols(j, t):
            return pl.ds(pl.multiple_of(((dx + t) % 2) * fq + j * w, w), w)

        def h_dz(j, t):
            return rcopy(h.at[pl.ds(oth, ne), hcols(j, t)], h2.at[:, hcols(j, t)], hs.at[j, t], hr.at[j, t], to_dz)

        def start(cs):
            for c in cs:
                c.start()

        def wait_all(cs):
            for c in cs:
                c.wait()

        def wait_recv(cs):
            for c in cs:
                c.wait_recv()

        barrier = pltpu.get_barrier_semaphore()
        for dev in (to_dx, to_dy, to_dz):
            pl.semaphore_signal(barrier, inc=1, device_id=dev, device_id_type=MESH)
        pl.semaphore_wait(barrier, 3)

        for i in range(xc):
            x_dy(i).start()
        x_dz.start()
        x_lo.start()

        @pl.loop(0, la)
        def _(j):
            start(w_dy(j))

        for i in range(xc):
            x_dy(i).wait_recv()
            x_fw(i).start()
        for p in range(npr - 1):
            d2_dz(p).start()

        @pl.when(dx == 0)
        def _():
            d2_dz(npr - 1).start()

        start(bulk)
        x_lo.wait()
        first_d = pltpu.make_async_copy(wd.at[:, dcols(0)], dbuf.at[0], lds.at[8])
        first_d.start()
        x_dz.wait_recv()
        for i in range(xc):
            x_fw(i).wait_recv()
        wait_recv(bulk)

        def gate_up(row, j):
            rs = pl.ds(pl.multiple_of(row, tm), tm)
            xt = xg[rs, :]
            g = jnp.dot(xt, wbuf[0], preferred_element_type=F32).astype(BF16).astype(F32)
            u = jnp.dot(xt, wbuf[1], preferred_element_type=F32).astype(BF16).astype(F32)
            val = (g * jax.nn.sigmoid(g) * u).astype(BF16)
            for t in range(2):
                h[rs, hcols(j, t)] = val[:, t * w:(t + 1) * w]

        def rest(j):
            @pl.loop(0, nz + 1)
            def _(i):
                gate_up((i + (i + nz) // (nz + 1)) * tm, j)

                @pl.when(i == 1)
                def _():
                    h_dz(j, 0).start()
                    h_dz(j, 1).start()

        @pl.loop(0, nc)
        def _(j):
            @pl.when(j + la < nc)
            def _():
                start(w_dy(j + la))

            @pl.when(jnp.logical_and(j >= la, j < la + npr))
            def _():
                d_dy(j - la).start()

            @pl.when(jnp.logical_and(j >= nc - npr - 1, j < nc - 2))
            def _():
                p = j - (nc - npr - 1)
                d2_dz(p).wait_recv()
                d2_fw(p).start()

            @pl.when(jnp.logical_and(dx == 0, j == nc - 2))
            def _():
                d2_dz(npr - 1).wait_recv()
                d2_fw(npr - 1).start()

            wait_recv(w_dy(j))
            start(w_fw(j))
            la_, lb_ = pl.ds(0, w), pl.ds(w, w)
            ld0 = [pltpu.make_async_copy(wg.at[:, cols(j)], wbuf.at[0, left, la_], lds.at[0]),
                   pltpu.make_async_copy(wu.at[:, cols(j)], wbuf.at[1, left, la_], lds.at[1]),
                   pltpu.make_async_copy(wpo.at[0, :, cols(j)], wbuf.at[0, left, lb_], lds.at[2]),
                   pltpu.make_async_copy(wpo.at[1, :, cols(j)], wbuf.at[1, left, lb_], lds.at[3]),
                   pltpu.make_async_copy(wdy.at[j, 0], wbuf.at[0, right, la_], lds.at[4]),
                   pltpu.make_async_copy(wdy.at[j, 1], wbuf.at[1, right, la_], lds.at[5])]
            ld1 = [pltpu.make_async_copy(wpx.at[j, 0], wbuf.at[0, right, lb_], lds.at[6]),
                   pltpu.make_async_copy(wpx.at[j, 1], wbuf.at[1, right, lb_], lds.at[7])]
            start(ld0)
            wait_recv(w_fw(j))
            start(ld1)
            wait_all(ld0 + ld1)
            gate_up(oth + (nz - 1) * tm, j)

            @pl.when(j < nc - 1)
            def _():
                rest(j)

        def split(k):
            late = (k + nk - nl) // nk
            s = (k - nl) // nz
            last = s // (2 * npr)
            odd = k // (nl - 1)
            half = late * (1 - last)
            p = (1 - late) * (k // 2) + late * ((1 - last) * (s // 2) + last * (npr - 1))
            q = (1 - late) * ((1 - odd) * (k % 2) + odd * dx) + late * ((1 - last) * (s % 2) + last * (1 - dx))
            r = (1 - late) * (nz - 1) + late * ((k - nl) % nz)
            return half, p, q, r

        def chunk_src(half, p, q):
            if half == 0:
                return (wd, dpo)[q].at[:, dcols(p)]
            return (ddy, dpx)[q].at[p]

        def load_d(k, slot, ok):
            half, p, q, r = split(k)
            ok = jnp.logical_and(ok, jnp.logical_or(k < nl, r == 0))
            for hh in range(2):
                for qq in range(2):
                    @pl.when(jnp.logical_and(ok, jnp.logical_and(half == hh, q == qq)))
                    def _(hh=hh, qq=qq):
                        c = pltpu.make_async_copy(chunk_src(hh, p, qq), dbuf.at[slot], lds.at[slot])
                        c.start()
                        c.wait()

        def z_send(k):
            return rcopy(zs.at[k % (lag + 1)], zr.at[k], zss.at[k], zsr.at[k], to_dz)

        def out_cols(p, q):
            return pl.ds(pl.multiple_of(((dx + q) % 2) * dq + p * cw, cw), cw)

        def out_at(m, base):
            half, p, q, r = split(m)
            return z.at[pl.ds(pl.multiple_of(base + r * tm, tm), tm), out_cols(p, q)]

        def is_other(m):
            return split(m)[0] == 1

        def out_local(m):
            return pltpu.make_async_copy(zo.at[m % 2], out_at(m, mine), zls.at[m % 2])

        def out_remote(m):
            i = m - nl
            return rcopy(zo.at[m % 2], out_at(m, mine), zos.at[i], zor.at[i], to_dy)

        def in_remote(m):
            i = m - nl
            return rcopy(zo.at[m % 2], out_at(m, theirs), zos.at[i], zor.at[i], to_dy)

        def free_out(m):
            @pl.when(is_other(m))
            def _():
                out_remote(m).wait_send()

            @pl.when(jnp.logical_not(is_other(m)))
            def _():
                out_local(m).wait()

        def send_piece(k):
            half, p, q, r = split(k)

            @pl.when(jnp.logical_and(jnp.logical_and(half == 1, q == 1), r == 0))
            def _():
                d_fw(p).wait_recv()

            @pl.when(k == 0)
            def _():
                first_d.wait()

            load_d(k, 0, k > 0)

            @pl.when(k > lag)
            def _():
                z_send(k - lag - 1).wait_send()

            zs[k % (lag + 1)] = jnp.dot(h[pl.ds(pl.multiple_of(oth + r * tm, tm), tm), :], dbuf[0],
                                        preferred_element_type=F32)
            z_send(k).start()

        def e_out(e):
            _, p, q, _ = split(e)
            return pltpu.make_async_copy(zo.at[2], z.at[pl.ds(mine, ne), out_cols(p, q)], zls.at[2])

        def e_piece(e):
            _, p, q, _ = split(e)
            for qq in range(2):
                @pl.when(q == qq)
                def _(qq=qq):
                    c = [pltpu.make_async_copy(chunk_src(0, p, qq), dbuf.at[2], lds.at[2]),
                         pltpu.make_async_copy((d2o, d2p)[qq].at[p], dbuf.at[3], lds.at[3])]
                    start(c)
                    wait_all(c)

            acc = jnp.dot(h[pl.ds(own, ne), :], dbuf[2], preferred_element_type=F32)
            acc = acc + jnp.dot(h2[...], dbuf[3], preferred_element_type=F32)

            @pl.when(e >= 1)
            def _():
                e_out(e - 1).wait()

            zo[2] = acc.astype(BF16)
            e_out(e).start()

        e0 = 7

        @pl.loop(0, nk + lag)
        def _(k):
            @pl.when(k < nk)
            def _():
                send_piece(k)

            @pl.when(k == lag - 1)
            def _():
                rest(nc - 1)

            f = k - (nl - 1)

            @pl.when(jnp.logical_and(f >= 0, jnp.logical_and(f < 2 * nz * npr, f % (2 * nz) == 0)))
            def _():
                d_dy(f // (2 * nz)).wait_recv()
                d_fw(f // (2 * nz)).start()

            @pl.when(k == e0 - 1)
            def _():
                for p in range(npr - 1):
                    d2_fw(p).wait_recv()

                @pl.when(dx == 1)
                def _():
                    d2_fw(npr - 1).wait_recv()

                @pl.loop(0, nc)
                def _(j):
                    for t in range(2):
                        h_dz(j, t).wait_recv()

            @pl.when(jnp.logical_and(k >= e0, jnp.logical_and(k < e0 + 2 * nl, (k - e0) % 2 == 0)))
            def _():
                e_piece((k - e0) // 2)

            @pl.when(k >= lag)
            def _():
                m = k - lag
                half, p, q, r = split(m)
                load_d(m, 1, k >= lag)
                zacc[...] = jnp.dot(h[pl.ds(pl.multiple_of(own + r * tm, tm), tm), :], dbuf[1],
                                    preferred_element_type=F32)

                @pl.when(m >= 2)
                def _():
                    free_out(m - 2)

                z_send(m).wait_recv()
                c = pltpu.make_async_copy(zr.at[m], zin, lds.at[4])
                c.start()
                c.wait()
                zo[m % 2] = (zacc[...] + zin[...]).astype(BF16)

                @pl.when(half == 0)
                def _():
                    out_local(m).start()

                @pl.when(half == 1)
                def _():
                    out_remote(m).start()

        for m in (nk - 2, nk - 1):
            out_local(m).wait()
        e_out(nl - 1).wait()
        for k in range(nk - lag - 1, nk):
            z_send(k).wait_send()
        for i in range(xc):
            x_dy(i).wait_send()
            x_fw(i).wait_send()
        x_dz.wait_send()

        @pl.loop(0, nc)
        def _(j):
            for c in w_dy(j) + w_fw(j) + [h_dz(j, 0), h_dz(j, 1)]:
                c.wait_send()

        @pl.loop(0, npr)
        def _(p):
            d_dy(p).wait_send()
            d_fw(p).wait_send()

        for c in bulk:
            c.wait_send()
        for p in range(npr - 1):
            d2_dz(p).wait_send()
            d2_fw(p).wait_send()

        @pl.when(dx == 0)
        def _():
            d2_dz(npr - 1).wait_send()
            d2_fw(npr - 1).wait_send()

        @pl.loop(nl, nl + no)
        def _(m):
            in_remote(m).wait_recv()

    def sd(shape, dtype=BF16):
        return jax.ShapeDtypeStruct(shape, dtype)

    wl, dl = sd((nc, 2, dh, w)), sd((npr, fh, cw))
    outs = (sd((rows, dh)), wl, sd((2, dh, fq)), wl, dl, sd((fh, dq)), dl, dl, dl, sd((nk, tm, cw), F32))
    dma = pltpu.SemaphoreType.DMA
    return pl.pallas_call(
        kernel,
        out_shape=outs,
        in_specs=[pl.BlockSpec(memory_space=pl.ANY)] * 4,
        out_specs=[pl.BlockSpec(memory_space=pl.ANY)] * len(outs),
        scratch_shapes=[
            pltpu.VMEM((rows, 2 * dh), BF16),
            pltpu.VMEM((rows, fh), BF16),
            pltpu.VMEM((ne, fh), BF16),
            pltpu.VMEM((2, 2 * dh, 2 * w), BF16),
            pltpu.VMEM((4, fh, cw), BF16),
            pltpu.VMEM((lag + 1, tm, cw), F32),
            pltpu.VMEM((tm, cw), F32),
            pltpu.VMEM((tm, cw), F32),
            pltpu.VMEM((3, tm, cw), BF16),
            dma((2 * xc + 1,)), dma((2 * xc + 1,)),
            dma((nc, 2)), dma((nc, 2)), dma((nc, 2)), dma((nc, 2)), dma((nc, 2)), dma((nc, 2)), dma((3,)), dma((3,)),
            dma((npr,)), dma((npr,)), dma((npr,)), dma((npr,)), dma((npr,)), dma((npr,)), dma((npr,)), dma((npr,)),
            dma((nk,)), dma((nk,)), dma((no,)), dma((no,)), dma((3,)), dma((9,)),
        ],
        compiler_params=pltpu.CompilerParams(
            collective_id=0, has_side_effects=True, vmem_limit_bytes=62 * 1024 * 1024),
    )


def solution(mesh):
    x_spec = P(("grp", "dx", "dz"), "dy")
    w_in_spec = P("dy", ("dz", "dx"))
    w_out_spec = P("dz", ("dy", "dx"))

    def local_mlp(x_blk, wg_blk, wu_blk, wd_blk):
        return make_local_mlp(x_blk.shape, wg_blk.shape, wd_blk.shape)(x_blk, wg_blk, wu_blk, wd_blk)[0]

    return jax.shard_map(local_mlp, mesh=mesh, in_specs=(x_spec, w_in_spec, w_in_spec, w_out_spec), out_specs=x_spec, check_vma=False)
```

time: 600 us -> 589 us (0.982)
  Pallas kernels: 592 us -> 581 us
    pallas_call x1, Pallas kernels: 592 us -> 581 us  [local_mlp(): make_local_mlp(x_blk.shape, wg_blk.shape, wd_blk.shape)]
where the time goes in v3:
time: 589 us; the launch traced here: 587 us
  Pallas kernels  581 us (99%)
  local copies, waits for them, and re-layouts  5.89 us (1%)
    pallas_call x1, Pallas kernels, local_mlp(): make_local_mlp(x_blk.shape, wg_blk.shape, wd_blk.shape)  581 us

profile of v3, /device:TPU:0, one launch (start us, length us, event | category | flops | bytes accessed | tf_op | source)
XLA Modules:
  0.0 586.8 jit_solution(5232306240864183975)
XLA Ops:
  0.0 580.9 %shard_map.46 = (bf16[2048,1536]{1,0:T(8,128)(2,1)}, bf16[16,2,1536,128]{3,2,1,0:T(8,128)(2,1)}, bf16[2,1536,2048]{2,1,0:T(8,128)(2,1)}, bf16[16,2,1536,128]{3,2...) custom-call(bf16[2048,1536]{1,0:T(8,128)(2,1)} %x.1, ...), custom_call_target="tpu_custom_call" | custom-call | tf_op jit(solution)/shard_map/pallas_call | solution.py:446
  580.9 5.9 %copy.6 = bf16[2048,1536]{1,0:T(8,128)(2,1)} copy(bf16[2048,1536]{1,0:T(8,128)(2,1)} %get-tuple-element.6) | data formatting | bytes 12582912

commit v4 on v3

--- a/solution.py
+++ b/solution.py
@@ -17,6 +17,7 @@
     ra = rows // 2
     w = 128
     nc = fq // w
+    na = 4
     la = 8
     cw = 256
     npr = dq // cw
@@ -118,6 +119,7 @@
             x_dy(i).start()
         x_dz.start()
         x_lo.start()
+        start(bulk[:2])
 
         @pl.loop(0, la)
         def _(j):
@@ -133,14 +135,11 @@
         def _():
             d2_dz(npr - 1).start()
 
-        start(bulk)
+        bulk[2].start()
         x_lo.wait()
         first_d = pltpu.make_async_copy(wd.at[:, dcols(0)], dbuf.at[0], lds.at[8])
         first_d.start()
-        x_dz.wait_recv()
-        for i in range(xc):
-            x_fw(i).wait_recv()
-        wait_recv(bulk)
+        wait_recv(bulk[:2])
 
         def gate_up(row, j):
             rs = pl.ds(pl.multiple_of(row, tm), tm)
@@ -161,12 +160,58 @@
                     h_dz(j, 0).start()
                     h_dz(j, 1).start()
 
-        @pl.loop(0, nc)
+        lc, rc = pl.ds(0, w), pl.ds(w, w)
+
+        def loads(j):
+            return [pltpu.make_async_copy(wg.at[:, cols(j)], wbuf.at[0, left, lc], lds.at[0]),
+                    pltpu.make_async_copy(wu.at[:, cols(j)], wbuf.at[1, left, lc], lds.at[1]),
+                    pltpu.make_async_copy(wpo.at[0, :, cols(j)], wbuf.at[0, left, rc], lds.at[2]),
+                    pltpu.make_async_copy(wpo.at[1, :, cols(j)], wbuf.at[1, left, rc], lds.at[3]),
+                    pltpu.make_async_copy(wdy.at[j, 0], wbuf.at[0, right, lc], lds.at[4]),
+                    pltpu.make_async_copy(wdy.at[j, 1], wbuf.at[1, right, lc], lds.at[5]),
+                    pltpu.make_async_copy(wpx.at[j, 0], wbuf.at[0, right, rc], lds.at[6]),
+                    pltpu.make_async_copy(wpx.at[j, 1], wbuf.at[1, right, rc], lds.at[7])]
+
+        def arrive(j):
+            @pl.when(j + la < nc)
+            def _():
+                start(w_dy(j + la))
+
+            wait_recv(w_dy(j))
+            start(w_fw(j))
+            ld = loads(j)
+            start(ld[:6])
+            wait_recv(w_fw(j))
+            start(ld[6:])
+            wait_all(ld)
+
+        @pl.loop(0, na)
         def _(j):
-            @pl.when(j + la < nc)
-            def _():
-                start(w_dy(j + la))
-
+            arrive(j)
+
+            @pl.loop(0, nz)
+            def _(i):
+                gate_up(own + i * tm, j)
+
+        x_dz.wait_recv()
+        for i in range(xc):
+            x_fw(i).wait_recv()
+
+        @pl.loop(0, na)
+        def _(j):
+            ld = loads(j)
+            start(ld)
+            wait_all(ld)
+
+            @pl.loop(0, nz)
+            def _(i):
+                gate_up(oth + i * tm, j)
+
+            h_dz(j, 0).start()
+            h_dz(j, 1).start()
+
+        @pl.loop(na, nc)
+        def _(j):
             @pl.when(jnp.logical_and(j >= la, j < la + npr))
             def _():
                 d_dy(j - la).start()
@@ -182,26 +227,14 @@
                 d2_dz(npr - 1).wait_recv()
                 d2_fw(npr - 1).start()
 
-            wait_recv(w_dy(j))
-            start(w_fw(j))
-            la_, lb_ = pl.ds(0, w), pl.ds(w, w)
-            ld0 = [pltpu.make_async_copy(wg.at[:, cols(j)], wbuf.at[0, left, la_], lds.at[0]),
-                   pltpu.make_async_copy(wu.at[:, cols(j)], wbuf.at[1, left, la_], lds.at[1]),
-                   pltpu.make_async_copy(wpo.at[0, :, cols(j)], wbuf.at[0, left, lb_], lds.at[2]),
-                   pltpu.make_async_copy(wpo.at[1, :, cols(j)], wbuf.at[1, left, lb_], lds.at[3]),
-                   pltpu.make_async_copy(wdy.at[j, 0], wbuf.at[0, right, la_], lds.at[4]),
-                   pltpu.make_async_copy(wdy.at[j, 1], wbuf.at[1, right, la_], lds.at[5])]
-            ld1 = [pltpu.make_async_copy(wpx.at[j, 0], wbuf.at[0, right, lb_], lds.at[6]),
-                   pltpu.make_async_copy(wpx.at[j, 1], wbuf.at[1, right, lb_], lds.at[7])]
-            start(ld0)
-            wait_recv(w_fw(j))
-            start(ld1)
-            wait_all(ld0 + ld1)
+            arrive(j)
             gate_up(oth + (nz - 1) * tm, j)
 
             @pl.when(j < nc - 1)
             def _():
                 rest(j)
+
+        bulk[2].wait_recv()
 
         def split(k):
             late = (k + nk - nl) // nk

time: 589 us -> 589 us (level)
  no operation moved by 1% of the time
where the time goes in v4:
time: 589 us; the launch traced here: 587 us
  Pallas kernels  581 us (99%)
  local copies, waits for them, and re-layouts  5.89 us (1%)
    pallas_call x1, Pallas kernels, local_mlp(): make_local_mlp(x_blk.shape, wg_blk.shape, wd_blk.shape)  581 us

profile of v4, /device:TPU:0, one launch (start us, length us, event | category | flops | bytes accessed | tf_op | source)
XLA Modules:
  0.0 586.8 jit_solution(212714451044572892)
XLA Ops:
  0.0 580.9 %shard_map.46 = (bf16[2048,1536]{1,0:T(8,128)(2,1)}, bf16[16,2,1536,128]{3,2,1,0:T(8,128)(2,1)}, bf16[2,1536,2048]{2,1,0:T(8,128)(2,1)}, bf16[16,2,1536,128]{3,2...) custom-call(bf16[2048,1536]{1,0:T(8,128)(2,1)} %x.1, ...), custom_call_target="tpu_custom_call" | custom-call | tf_op jit(solution)/shard_map/pallas_call | solution.py:479
  580.9 5.9 %copy.6 = bf16[2048,1536]{1,0:T(8,128)(2,1)} copy(bf16[2048,1536]{1,0:T(8,128)(2,1)} %get-tuple-element.6) | data formatting | bytes 12582912

commit v5 on v4

--- a/solution.py
+++ b/solution.py
@@ -27,14 +27,15 @@
     nl = 2 * npr - 1
     nk = nl + nz * (4 * npr - nl)
     no = nz * 2 * npr
-    lag = 3
+    lag = 4
+    oslots = 8
     xc = 2
     xrc = ra // xc
     own, oth = ra, 0
 
     def kernel(x, wg, wu, wd,
-               z, wdy, wpo, wpx, ddy, dpo, dpx, d2o, d2p, zr,
-               xg, h, h2, wbuf, dbuf, zs, zin, zacc, zo,
+               z, wdy, wpo, wpx, ddy, dpo, dpx, d2o, d2p,
+               xg, h, h2, wbuf, dbuf, zs, zr, zacc, zo,
                xs, xr, wys, wyr, wfs, wfr, hs, hr, bs, br,
                dys, dyr, dfs, dfr, d2s, d2r, d2t, d2u,
                zss, zsr, zos, zor, zls, lds):
@@ -277,15 +278,15 @@
             return split(m)[0] == 1
 
         def out_local(m):
-            return pltpu.make_async_copy(zo.at[m % 2], out_at(m, mine), zls.at[m % 2])
+            return pltpu.make_async_copy(zo.at[m % oslots], out_at(m, mine), zls.at[m % oslots])
 
         def out_remote(m):
             i = m - nl
-            return rcopy(zo.at[m % 2], out_at(m, mine), zos.at[i], zor.at[i], to_dy)
+            return rcopy(zo.at[m % oslots], out_at(m, mine), zos.at[i], zor.at[i], to_dy)
 
         def in_remote(m):
             i = m - nl
-            return rcopy(zo.at[m % 2], out_at(m, theirs), zos.at[i], zor.at[i], to_dy)
+            return rcopy(zo.at[m % oslots], out_at(m, theirs), zos.at[i], zor.at[i], to_dy)
 
         def free_out(m):
             @pl.when(is_other(m))
@@ -319,7 +320,7 @@
 
         def e_out(e):
             _, p, q, _ = split(e)
-            return pltpu.make_async_copy(zo.at[2], z.at[pl.ds(mine, ne), out_cols(p, q)], zls.at[2])
+            return pltpu.make_async_copy(zo.at[oslots], z.at[pl.ds(mine, ne), out_cols(p, q)], zls.at[oslots])
 
         def e_piece(e):
             _, p, q, _ = split(e)
@@ -338,7 +339,7 @@
             def _():
                 e_out(e - 1).wait()
 
-            zo[2] = acc.astype(BF16)
+            zo[oslots] = acc.astype(BF16)
             e_out(e).start()
 
         e0 = 7
@@ -386,15 +387,12 @@
                 zacc[...] = jnp.dot(h[pl.ds(pl.multiple_of(own + r * tm, tm), tm), :], dbuf[1],
                                     preferred_element_type=F32)
 
-                @pl.when(m >= 2)
+                @pl.when(m >= oslots)
                 def _():
-                    free_out(m - 2)
+                    free_out(m - oslots)
 
                 z_send(m).wait_recv()
-                c = pltpu.make_async_copy(zr.at[m], zin, lds.at[4])
-                c.start()
-                c.wait()
-                zo[m % 2] = (zacc[...] + zin[...]).astype(BF16)
+                zo[m % oslots] = (zacc[...] + zr[m]).astype(BF16)
 
                 @pl.when(half == 0)
                 def _():
@@ -404,8 +402,10 @@
                 def _():
                     out_remote(m).start()
 
-        for m in (nk - 2, nk - 1):
-            out_local(m).wait()
+        @pl.loop(nk - oslots, nk)
+        def _(m):
+            free_out(m)
+
         e_out(nl - 1).wait()
         for k in range(nk - lag - 1, nk):
             z_send(k).wait_send()
@@ -443,7 +443,7 @@
         return jax.ShapeDtypeStruct(shape, dtype)
 
     wl, dl = sd((nc, 2, dh, w)), sd((npr, fh, cw))
-    outs = (sd((rows, dh)), wl, sd((2, dh, fq)), wl, dl, sd((fh, dq)), dl, dl, dl, sd((nk, tm, cw), F32))
+    outs = (sd((rows, dh)), wl, sd((2, dh, fq)), wl, dl, sd((fh, dq)), dl, dl, dl)
     dma = pltpu.SemaphoreType.DMA
     return pl.pallas_call(
         kernel,
@@ -457,13 +457,13 @@
             pltpu.VMEM((2, 2 * dh, 2 * w), BF16),
             pltpu.VMEM((4, fh, cw), BF16),
             pltpu.VMEM((lag + 1, tm, cw), F32),
+            pltpu.VMEM((nk, tm, cw), F32),
             pltpu.VMEM((tm, cw), F32),
-            pltpu.VMEM((tm, cw), F32),
-            pltpu.VMEM((3, tm, cw), BF16),
+            pltpu.VMEM((oslots + 1, tm, cw), BF16),
             dma((2 * xc + 1,)), dma((2 * xc + 1,)),
             dma((nc, 2)), dma((nc, 2)), dma((nc, 2)), dma((nc, 2)), dma((nc, 2)), dma((nc, 2)), dma((3,)), dma((3,)),
             dma((npr,)), dma((npr,)), dma((npr,)), dma((npr,)), dma((npr,)), dma((npr,)), dma((npr,)), dma((npr,)),
-            dma((nk,)), dma((nk,)), dma((no,)), dma((no,)), dma((3,)), dma((9,)),
+            dma((nk,)), dma((nk,)), dma((no,)), dma((no,)), dma((oslots + 1,)), dma((9,)),
         ],
         compiler_params=pltpu.CompilerParams(
             collective_id=0, has_side_effects=True, vmem_limit_bytes=62 * 1024 * 1024),

time: 589 us -> 580 us (0.985)
  Pallas kernels: 581 us -> 573 us
    pallas_call x1, Pallas kernels: 581 us -> 573 us  [local_mlp(): make_local_mlp(x_blk.shape, wg_blk.shape, wd_blk.shape)]
where the time goes in v5:
time: 580 us; the launch traced here: 579 us
  Pallas kernels  573 us (99%)
  local copies, waits for them, and re-layouts  5.89 us (1%)
    pallas_call x1, Pallas kernels, local_mlp(): make_local_mlp(x_blk.shape, wg_blk.shape, wd_blk.shape)  573 us

profile of v5, /device:TPU:0, one launch (start us, length us, event | category | flops | bytes accessed | tf_op | source)
XLA Modules:
  0.0 578.9 jit_solution(13632291257766293221)
XLA Ops:
  0.0 573.0 %shard_map.46 = (bf16[2048,1536]{1,0:T(8,128)(2,1)}, bf16[16,2,1536,128]{3,2,1,0:T(8,128)(2,1)}, bf16[2,1536,2048]{2,1,0:T(8,128)(2,1)}, bf16[16,2,1536,128]{3,2...) custom-call(bf16[2048,1536]{1,0:T(8,128)(2,1)} %x.1, ...), custom_call_target="tpu_custom_call" | custom-call | tf_op jit(solution)/shard_map/pallas_call | solution.py:479
  573.0 5.9 %copy.6 = bf16[2048,1536]{1,0:T(8,128)(2,1)} copy(bf16[2048,1536]{1,0:T(8,128)(2,1)} %get-tuple-element.6) | data formatting | bytes 12582912

commit v6 on v5

--- a/solution.py
+++ b/solution.py
@@ -23,7 +23,8 @@
     npr = dq // cw
     tm = 512
     nz = ra // tm
-    ne = tm
+    ne = tm + 64
+    nn = ra - ne
     nl = 2 * npr - 1
     nk = nl + nz * (4 * npr - nl)
     no = nz * 2 * npr
@@ -35,7 +36,7 @@
 
     def kernel(x, wg, wu, wd,
                z, wdy, wpo, wpx, ddy, dpo, dpx, d2o, d2p,
-               xg, h, h2, wbuf, dbuf, zs, zr, zacc, zo,
+               xg, h, h2, wbuf, wlast, dbuf, zs, zr, zacc, zo, zoe,
                xs, xr, wys, wyr, wfs, wfr, hs, hr, bs, br,
                dys, dyr, dfs, dfr, d2s, d2r, d2t, d2u,
                zss, zsr, zos, zor, zls, lds):
@@ -75,6 +76,16 @@
         def w_fw(j):
             return [rcopy(wdy.at[j, t], wpx.at[j, t], wfs.at[j, t], wfr.at[j, t], to_dx) for t in range(2)]
 
+        lc, rc = pl.ds(0, w), pl.ds(w, w)
+        jl = nc - 1
+        w_dy_last = [rcopy(src.at[:, pl.ds(jl * w, w)], wlast.at[t, right, lc], wys.at[jl, t], wyr.at[jl, t], to_dy)
+                     for t, src in enumerate((wg, wu))]
+        w_fw_last = [rcopy(wlast.at[t, right, lc], wlast.at[t, right, rc], wfs.at[jl, t], wfr.at[jl, t], to_dx)
+                     for t in range(2)]
+        ld_last = [pltpu.make_async_copy(src.at[:, pl.ds(jl * w, w)], wlast.at[t, left, c], lds.at[9 + 2 * i + t])
+                   for i, (srcs, c) in enumerate((((wg, wu), lc), ((wpo.at[0], wpo.at[1]), rc)))
+                   for t, src in enumerate(srcs)]
+
         def dcols(p):
             return pl.ds(pl.multiple_of(p * cw, cw), cw)
 
@@ -142,26 +153,26 @@
         first_d.start()
         wait_recv(bulk[:2])
 
-        def gate_up(row, j):
-            rs = pl.ds(pl.multiple_of(row, tm), tm)
+        def gate_up(row, n, j, wb):
+            rs = pl.ds(pl.multiple_of(row, 64), n)
             xt = xg[rs, :]
-            g = jnp.dot(xt, wbuf[0], preferred_element_type=F32).astype(BF16).astype(F32)
-            u = jnp.dot(xt, wbuf[1], preferred_element_type=F32).astype(BF16).astype(F32)
+            g = jnp.dot(xt, wb[0], preferred_element_type=F32).astype(BF16).astype(F32)
+            u = jnp.dot(xt, wb[1], preferred_element_type=F32).astype(BF16).astype(F32)
             val = (g * jax.nn.sigmoid(g) * u).astype(BF16)
             for t in range(2):
                 h[rs, hcols(j, t)] = val[:, t * w:(t + 1) * w]
 
-        def rest(j):
-            @pl.loop(0, nz + 1)
+        def rest(j, wb):
+            gate_up(oth, ne, j, wb)
+
+            @pl.loop(0, nz)
             def _(i):
-                gate_up((i + (i + nz) // (nz + 1)) * tm, j)
-
-                @pl.when(i == 1)
+                gate_up(own + i * tm, tm, j, wb)
+
+                @pl.when(i == 0)
                 def _():
                     h_dz(j, 0).start()
                     h_dz(j, 1).start()
-
-        lc, rc = pl.ds(0, w), pl.ds(w, w)
 
         def loads(j):
             return [pltpu.make_async_copy(wg.at[:, cols(j)], wbuf.at[0, left, lc], lds.at[0]),
@@ -174,9 +185,13 @@
                     pltpu.make_async_copy(wpx.at[j, 1], wbuf.at[1, right, rc], lds.at[7])]
 
         def arrive(j):
-            @pl.when(j + la < nc)
+            @pl.when(j + la < jl)
             def _():
                 start(w_dy(j + la))
+
+            @pl.when(j + la == jl)
+            def _():
+                start(w_dy_last)
 
             wait_recv(w_dy(j))
             start(w_fw(j))
@@ -192,8 +207,9 @@
 
             @pl.loop(0, nz)
             def _(i):
-                gate_up(own + i * tm, j)
-
+                gate_up(own + i * tm, tm, j, wbuf)
+
+        start(ld_last)
         x_dz.wait_recv()
         for i in range(xc):
             x_fw(i).wait_recv()
@@ -204,14 +220,12 @@
             start(ld)
             wait_all(ld)
 
-            @pl.loop(0, nz)
-            def _(i):
-                gate_up(oth + i * tm, j)
-
+            gate_up(oth, ne, j, wbuf)
+            gate_up(oth + ne, nn, j, wbuf)
             h_dz(j, 0).start()
             h_dz(j, 1).start()
 
-        @pl.loop(na, nc)
+        @pl.loop(na, jl)
         def _(j):
             @pl.when(jnp.logical_and(j >= la, j < la + npr))
             def _():
@@ -229,12 +243,14 @@
                 d2_fw(npr - 1).start()
 
             arrive(j)
-            gate_up(oth + (nz - 1) * tm, j)
-
-            @pl.when(j < nc - 1)
-            def _():
-                rest(j)
-
+            gate_up(oth + ne, nn, j, wbuf)
+            rest(j, wbuf)
+
+        wait_all(ld_last)
+        wait_recv(w_dy_last)
+        start(w_fw_last)
+        wait_recv(w_fw_last)
+        gate_up(oth + ne, nn, jl, wlast)
         bulk[2].wait_recv()
 
         def split(k):
@@ -264,8 +280,19 @@
                         c.start()
                         c.wait()
 
-        def z_send(k):
-            return rcopy(zs.at[k % (lag + 1)], zr.at[k], zss.at[k], zsr.at[k], to_dz)
+        def sized(k, fn):
+            _, _, _, r = split(k)
+
+            @pl.when(k < nl)
+            def _():
+                fn(ne, nn)
+
+            @pl.when(k >= nl)
+            def _():
+                fn(pl.multiple_of(r * tm, tm), tm)
+
+        def z_send(k, n):
+            return rcopy(zs.at[k % (lag + 1), pl.ds(0, n)], zr.at[k, pl.ds(0, n)], zss.at[k], zsr.at[k], to_dz)
 
         def out_cols(p, q):
             return pl.ds(pl.multiple_of(((dx + q) % 2) * dq + p * cw, cw), cw)
@@ -277,8 +304,11 @@
         def is_other(m):
             return split(m)[0] == 1
 
-        def out_local(m):
-            return pltpu.make_async_copy(zo.at[m % oslots], out_at(m, mine), zls.at[m % oslots])
+        def out_local(m, row, n):
+            _, p, q, _ = split(m)
+            return pltpu.make_async_copy(zo.at[m % oslots, pl.ds(0, n)],
+                                         z.at[pl.ds(pl.multiple_of(mine + row, 64), n), out_cols(p, q)],
+                                         zls.at[m % oslots])
 
         def out_remote(m):
             i = m - nl
@@ -295,7 +325,7 @@
 
             @pl.when(jnp.logical_not(is_other(m)))
             def _():
-                out_local(m).wait()
+                sized(m, lambda row, n: out_local(m, row, n).wait())
 
         def send_piece(k):
             half, p, q, r = split(k)
@@ -312,15 +342,18 @@
 
             @pl.when(k > lag)
             def _():
-                z_send(k - lag - 1).wait_send()
-
-            zs[k % (lag + 1)] = jnp.dot(h[pl.ds(pl.multiple_of(oth + r * tm, tm), tm), :], dbuf[0],
-                                        preferred_element_type=F32)
-            z_send(k).start()
+                sized(k - lag - 1, lambda row, n: z_send(k - lag - 1, n).wait_send())
+
+            def piece(row, n):
+                zs[k % (lag + 1), pl.ds(0, n)] = jnp.dot(h[pl.ds(pl.multiple_of(oth + row, 64), n), :], dbuf[0],
+                                                         preferred_element_type=F32)
+                z_send(k, n).start()
+
+            sized(k, piece)
 
         def e_out(e):
             _, p, q, _ = split(e)
-            return pltpu.make_async_copy(zo.at[oslots], z.at[pl.ds(mine, ne), out_cols(p, q)], zls.at[oslots])
+            return pltpu.make_async_copy(zoe, z.at[pl.ds(mine, ne), out_cols(p, q)], zls.at[oslots])
 
         def e_piece(e):
             _, p, q, _ = split(e)
@@ -339,7 +372,7 @@
             def _():
                 e_out(e - 1).wait()
 
-            zo[oslots] = acc.astype(BF16)
+            zoe[...] = acc.astype(BF16)
             e_out(e).start()
 
         e0 = 7
@@ -352,7 +385,7 @@
 
             @pl.when(k == lag - 1)
             def _():
-                rest(nc - 1)
+                rest(jl, wlast)
 
             f = k - (nl - 1)
 
@@ -384,19 +417,21 @@
                 m = k - lag
                 half, p, q, r = split(m)
                 load_d(m, 1, k >= lag)
-                zacc[...] = jnp.dot(h[pl.ds(pl.multiple_of(own + r * tm, tm), tm), :], dbuf[1],
-                                    preferred_element_type=F32)
-
                 @pl.when(m >= oslots)
                 def _():
                     free_out(m - oslots)
 
-                z_send(m).wait_recv()
-                zo[m % oslots] = (zacc[...] + zr[m]).astype(BF16)
+                def piece(row, n):
+                    zacc[pl.ds(0, n)] = jnp.dot(h[pl.ds(pl.multiple_of(own + row, 64), n), :], dbuf[1],
+                                                preferred_element_type=F32)
+                    z_send(m, n).wait_recv()
+                    zo[m % oslots, pl.ds(0, n)] = (zacc[pl.ds(0, n)] + zr[m, pl.ds(0, n)]).astype(BF16)
+
+                sized(m, piece)
 
                 @pl.when(half == 0)
                 def _():
-                    out_local(m).start()
+                    sized(m, lambda row, n: out_local(m, row, n).start())
 
                 @pl.when(half == 1)
                 def _():
@@ -408,13 +443,16 @@
 
         e_out(nl - 1).wait()
         for k in range(nk - lag - 1, nk):
-            z_send(k).wait_send()
+            z_send(k, tm).wait_send()
         for i in range(xc):
             x_dy(i).wait_send()
             x_fw(i).wait_send()
         x_dz.wait_send()
 
-        @pl.loop(0, nc)
+        for c in w_dy_last + w_fw_last + [h_dz(jl, 0), h_dz(jl, 1)]:
+            c.wait_send()
+
+        @pl.loop(0, jl)
         def _(j):
             for c in w_dy(j) + w_fw(j) + [h_dz(j, 0), h_dz(j, 1)]:
                 c.wait_send()
@@ -455,18 +493,20 @@
             pltpu.VMEM((rows, fh), BF16),
             pltpu.VMEM((ne, fh), BF16),
             pltpu.VMEM((2, 2 * dh, 2 * w), BF16),
+            pltpu.VMEM((2, 2 * dh, 2 * w), BF16),
             pltpu.VMEM((4, fh, cw), BF16),
             pltpu.VMEM((lag + 1, tm, cw), F32),
             pltpu.VMEM((nk, tm, cw), F32),
             pltpu.VMEM((tm, cw), F32),
-            pltpu.VMEM((oslots + 1, tm, cw), BF16),
+            pltpu.VMEM((oslots, tm, cw), BF16),
+            pltpu.VMEM((ne, cw), BF16),
             dma((2 * xc + 1,)), dma((2 * xc + 1,)),
             dma((nc, 2)), dma((nc, 2)), dma((nc, 2)), dma((nc, 2)), dma((nc, 2)), dma((nc, 2)), dma((3,)), dma((3,)),
             dma((npr,)), dma((npr,)), dma((npr,)), dma((npr,)), dma((npr,)), dma((npr,)), dma((npr,)), dma((npr,)),
-            dma((nk,)), dma((nk,)), dma((no,)), dma((no,)), dma((oslots + 1,)), dma((9,)),
+            dma((nk,)), dma((nk,)), dma((no,)), dma((no,)), dma((oslots + 1,)), dma((13,)),
         ],
         compiler_params=pltpu.CompilerParams(
-            collective_id=0, has_side_effects=True, vmem_limit_bytes=62 * 1024 * 1024),
+            collective_id=0, has_side_effects=True, vmem_limit_bytes=67043328),
     )
 
 

time: 580 us -> 572 us (0.986)
  Pallas kernels: 573 us -> 565 us
    pallas_call x1, Pallas kernels: 573 us -> 565 us  [local_mlp(): make_local_mlp(x_blk.shape, wg_blk.shape, wd_blk.shape)]
where the time goes in v6:
time: 572 us; the launch traced here: 570 us
  Pallas kernels  565 us (99%)
  local copies, waits for them, and re-layouts  5.89 us (1%)
    pallas_call x1, Pallas kernels, local_mlp(): make_local_mlp(x_blk.shape, wg_blk.shape, wd_blk.shape)  565 us

profile of v6, /device:TPU:0, one launch (start us, length us, event | category | flops | bytes accessed | tf_op | source)
XLA Modules:
  0.0 570.5 jit_solution(477327209410586186)
XLA Ops:
  0.0 564.6 %shard_map.46 = (bf16[2048,1536]{1,0:T(8,128)(2,1)}, bf16[16,2,1536,128]{3,2,1,0:T(8,128)(2,1)}, bf16[2,1536,2048]{2,1,0:T(8,128)(2,1)}, bf16[16,2,1536,128]{3,2...) custom-call(bf16[2048,1536]{1,0:T(8,128)(2,1)} %x.1, ...), custom_call_target="tpu_custom_call" | custom-call | tf_op jit(solution)/shard_map/pallas_call | solution.py:519
  564.6 5.9 %copy.6 = bf16[2048,1536]{1,0:T(8,128)(2,1)} copy(bf16[2048,1536]{1,0:T(8,128)(2,1)} %get-tuple-element.6) | data formatting | bytes 12582912

commit v7 on v6

--- a/solution.py
+++ b/solution.py
@@ -247,10 +247,27 @@
             rest(j, wbuf)
 
         wait_all(ld_last)
+        late_rows, late_part = pl.ds(oth + ne, nn), pl.ds(0, nn)
+        for t in range(2):
+            zs[1 + t, late_part] = jnp.dot(xg[late_rows, left], wlast[t, left], preferred_element_type=F32)
+        first_d.wait()
+        done = [(t * fq, fq - w) for t in range(2)]
+        last = [(t * fq + fq - w, w) for t in range(2)]
+
+        def z_sum(parts):
+            return sum(jnp.dot(h[late_rows, pl.ds(a, n)], dbuf[0, pl.ds(a, n)], preferred_element_type=F32)
+                       for a, n in parts)
+
+        zacc[late_part] = z_sum(done)
         wait_recv(w_dy_last)
         start(w_fw_last)
         wait_recv(w_fw_last)
-        gate_up(oth + ne, nn, jl, wlast)
+        xr_ = xg[late_rows, right]
+        g, u = [(zs[1 + t, late_part] + jnp.dot(xr_, wlast[t, right], preferred_element_type=F32)).astype(BF16).astype(F32)
+                for t in range(2)]
+        val = (g * jax.nn.sigmoid(g) * u).astype(BF16)
+        for t in range(2):
+            h[late_rows, hcols(jl, t)] = val[:, t * w:(t + 1) * w]
         bulk[2].wait_recv()
 
         def split(k):
@@ -334,11 +351,7 @@
             def _():
                 d_fw(p).wait_recv()
 
-            @pl.when(k == 0)
-            def _():
-                first_d.wait()
-
-            load_d(k, 0, k > 0)
+            load_d(k, 0, True)
 
             @pl.when(k > lag)
             def _():
@@ -377,9 +390,12 @@
 
         e0 = 7
 
+        zs[0, late_part] = zacc[late_part] + z_sum(last)
+        z_send(0, nn).start()
+
         @pl.loop(0, nk + lag)
         def _(k):
-            @pl.when(k < nk)
+            @pl.when(jnp.logical_and(k > 0, k < nk))
             def _():
                 send_piece(k)
 
@@ -510,12 +526,38 @@
     )
 
 
+def copy_rows(shape):
+    n = 8
+    rows = shape[0] // n
+
+    def kernel(src, dst, buf, rs, ws):
+        part = [pl.ds(i * rows, rows) for i in range(n)]
+        reads = [pltpu.make_async_copy(src.at[p], buf.at[p], rs.at[i]) for i, p in enumerate(part)]
+        writes = [pltpu.make_async_copy(buf.at[p], dst.at[p], ws.at[i]) for i, p in enumerate(part)]
+        for r in reads:
+            r.start()
+        for r, c in zip(reads, writes):
+            r.wait()
+            c.start()
+        for c in writes:
+            c.wait()
+
+    return pl.pallas_call(
+        kernel,
+        out_shape=jax.ShapeDtypeStruct(shape, BF16),
+        in_specs=[pl.BlockSpec(memory_space=pl.ANY)],
+        out_specs=pl.BlockSpec(memory_space=pl.ANY),
+        scratch_shapes=[pltpu.VMEM(shape, BF16), pltpu.SemaphoreType.DMA((n,)), pltpu.SemaphoreType.DMA((n,))],
+    )
+
+
 def solution(mesh):
     x_spec = P(("grp", "dx", "dz"), "dy")
     w_in_spec = P("dy", ("dz", "dx"))
     w_out_spec = P("dz", ("dy", "dx"))
 
     def local_mlp(x_blk, wg_blk, wu_blk, wd_blk):
-        return make_local_mlp(x_blk.shape, wg_blk.shape, wd_blk.shape)(x_blk, wg_blk, wu_blk, wd_blk)[0]
+        outs = make_local_mlp(x_blk.shape, wg_blk.shape, wd_blk.shape)(x_blk, wg_blk, wu_blk, wd_blk)
+        return copy_rows(x_blk.shape)(outs[0])
 
     return jax.shard_map(local_mlp, mesh=mesh, in_specs=(x_spec, w_in_spec, w_in_spec, w_out_spec), out_specs=x_spec, check_vma=False)

time: 572 us -> 571 us (level)
  local copies, waits for them, and re-layouts: 5.89 us -> 0 us
    unnamed x1 -> x0, local copies, waits for them, and re-layouts: 5.89 us -> none
where the time goes in v7:
time: 571 us; the launch traced here: 569 us
  Pallas kernels  569 us (100%)
    pallas_call x1, Pallas kernels, local_mlp(): make_local_mlp(x_blk.shape, wg_blk.shape, wd_blk.shape)  564 us

profile of v7, /device:TPU:0, one launch (start us, length us, event | category | flops | bytes accessed | tf_op | source)
XLA Modules:
  0.0 569.2 jit_solution(13909584546662600574)
XLA Ops:
  0.0 563.6 %shard_map.46 = (bf16[2048,1536]{1,0:T(8,128)(2,1)}, bf16[16,2,1536,128]{3,2,1,0:T(8,128)(2,1)}, bf16[2,1536,2048]{2,1,0:T(8,128)(2,1)}, bf16[16,2,1536,128]{3,2...) custom-call(bf16[2048,1536]{1,0:T(8,128)(2,1)} %x.1, ...), custom_call_target="tpu_custom_call" | custom-call | tf_op jit(solution)/shard_map/pallas_call | solution.py:560
  563.6 5.5 shard_map.47

commit v8 on v7

--- a/solution.py
+++ b/solution.py
@@ -28,18 +28,18 @@
     nl = 2 * npr - 1
     nk = nl + nz * (4 * npr - nl)
     no = nz * 2 * npr
-    lag = 4
-    oslots = 8
+    lag = 2
+    oslots = 5
     xc = 2
     xrc = ra // xc
     own, oth = ra, 0
 
     def kernel(x, wg, wu, wd,
                z, wdy, wpo, wpx, ddy, dpo, dpx, d2o, d2p,
-               xg, h, h2, wbuf, wlast, dbuf, zs, zr, zacc, zo, zoe,
+               xg, h, h2, wbuf, wlast, dbuf, zs, zr, zacc, zo,
                xs, xr, wys, wyr, wfs, wfr, hs, hr, bs, br,
                dys, dyr, dfs, dfr, d2s, d2r, d2t, d2u,
-               zss, zsr, zos, zor, zls, lds):
+               zss, zsr, zos, zor, lds):
         dz = lax.axis_index("dz")
         dy = lax.axis_index("dy")
         dx = lax.axis_index("dx")
@@ -315,34 +315,14 @@
             return pl.ds(pl.multiple_of(((dx + q) % 2) * dq + p * cw, cw), cw)
 
         def out_at(m, base):
-            half, p, q, r = split(m)
+            _, p, q, r = split(m)
             return z.at[pl.ds(pl.multiple_of(base + r * tm, tm), tm), out_cols(p, q)]
 
-        def is_other(m):
-            return split(m)[0] == 1
-
-        def out_local(m, row, n):
-            _, p, q, _ = split(m)
-            return pltpu.make_async_copy(zo.at[m % oslots, pl.ds(0, n)],
-                                         z.at[pl.ds(pl.multiple_of(mine + row, 64), n), out_cols(p, q)],
-                                         zls.at[m % oslots])
-
-        def out_remote(m):
-            i = m - nl
-            return rcopy(zo.at[m % oslots], out_at(m, mine), zos.at[i], zor.at[i], to_dy)
-
-        def in_remote(m):
-            i = m - nl
-            return rcopy(zo.at[m % oslots], out_at(m, theirs), zos.at[i], zor.at[i], to_dy)
-
-        def free_out(m):
-            @pl.when(is_other(m))
-            def _():
-                out_remote(m).wait_send()
-
-            @pl.when(jnp.logical_not(is_other(m)))
-            def _():
-                sized(m, lambda row, n: out_local(m, row, n).wait())
+        def out_remote(i):
+            return rcopy(zo.at[i % oslots], out_at(i + nl, mine), zos.at[i], zor.at[i], to_dy)
+
+        def in_remote(i):
+            return rcopy(zo.at[i % oslots], out_at(i + nl, theirs), zos.at[i], zor.at[i], to_dy)
 
         def send_piece(k):
             half, p, q, r = split(k)
@@ -364,29 +344,22 @@
 
             sized(k, piece)
 
-        def e_out(e):
-            _, p, q, _ = split(e)
-            return pltpu.make_async_copy(zoe, z.at[pl.ds(mine, ne), out_cols(p, q)], zls.at[oslots])
+        parts = [(i, 2 * dh * i, min(2 * dh, fh - 2 * dh * i)) for i in range(2)]
 
         def e_piece(e):
             _, p, q, _ = split(e)
             for qq in range(2):
                 @pl.when(q == qq)
                 def _(qq=qq):
-                    c = [pltpu.make_async_copy(chunk_src(0, p, qq), dbuf.at[2], lds.at[2]),
-                         pltpu.make_async_copy((d2o, d2p)[qq].at[p], dbuf.at[3], lds.at[3])]
+                    c = [pltpu.make_async_copy(src.at[pl.ds(a, n)], buf.at[i, pl.ds(0, n)], lds.at[2 + 2 * b + i])
+                         for b, (src, buf) in enumerate(((chunk_src(0, p, qq), wbuf), ((d2o, d2p)[qq].at[p], wlast)))
+                         for i, a, n in parts]
                     start(c)
                     wait_all(c)
 
-            acc = jnp.dot(h[pl.ds(own, ne), :], dbuf[2], preferred_element_type=F32)
-            acc = acc + jnp.dot(h2[...], dbuf[3], preferred_element_type=F32)
-
-            @pl.when(e >= 1)
-            def _():
-                e_out(e - 1).wait()
-
-            zoe[...] = acc.astype(BF16)
-            e_out(e).start()
+            acc = sum(jnp.dot(lhs[pl.ds(r0, ne), pl.ds(a, n)], buf[i, pl.ds(0, n)], preferred_element_type=F32)
+                      for lhs, r0, buf in ((h, own, wbuf), (h2, 0, wlast)) for i, a, n in parts)
+            z[pl.ds(mine, ne), out_cols(p, q)] = acc.astype(BF16)
 
         e0 = 7
 
@@ -412,6 +385,9 @@
 
             @pl.when(k == e0 - 1)
             def _():
+                for c in w_fw_last:
+                    c.wait_send()
+
                 for p in range(npr - 1):
                     d2_fw(p).wait_recv()
 
@@ -433,31 +409,36 @@
                 m = k - lag
                 half, p, q, r = split(m)
                 load_d(m, 1, k >= lag)
-                @pl.when(m >= oslots)
+                i = m - nl
+
+                @pl.when(jnp.logical_and(i >= oslots, i < no))
                 def _():
-                    free_out(m - oslots)
+                    out_remote(i - oslots).wait_send()
 
                 def piece(row, n):
                     zacc[pl.ds(0, n)] = jnp.dot(h[pl.ds(pl.multiple_of(own + row, 64), n), :], dbuf[1],
                                                 preferred_element_type=F32)
                     z_send(m, n).wait_recv()
-                    zo[m % oslots, pl.ds(0, n)] = (zacc[pl.ds(0, n)] + zr[m, pl.ds(0, n)]).astype(BF16)
+                    val = (zacc[pl.ds(0, n)] + zr[m, pl.ds(0, n)]).astype(BF16)
+
+                    @pl.when(half == 0)
+                    def _():
+                        z[pl.ds(pl.multiple_of(mine + row, 64), n), out_cols(p, q)] = val
+
+                    @pl.when(half == 1)
+                    def _():
+                        zo[jnp.maximum(i, 0) % oslots, pl.ds(0, n)] = val
 
                 sized(m, piece)
-
-                @pl.when(half == 0)
-                def _():
-                    sized(m, lambda row, n: out_local(m, row, n).start())
 
                 @pl.when(half == 1)
                 def _():
-                    out_remote(m).start()
-
-        @pl.loop(nk - oslots, nk)
-        def _(m):
-            free_out(m)
-
-        e_out(nl - 1).wait()
+                    out_remote(i).start()
+
+        @pl.loop(no - oslots, no)
+        def _(i):
+            out_remote(i).wait_send()
+
         for k in range(nk - lag - 1, nk):
             z_send(k, tm).wait_send()
         for i in range(xc):
@@ -465,7 +446,7 @@
             x_fw(i).wait_send()
         x_dz.wait_send()
 
-        for c in w_dy_last + w_fw_last + [h_dz(jl, 0), h_dz(jl, 1)]:
+        for c in w_dy_last + [h_dz(jl, 0), h_dz(jl, 1)]:
             c.wait_send()
 
         @pl.loop(0, jl)
@@ -489,65 +470,39 @@
             d2_dz(npr - 1).wait_send()
             d2_fw(npr - 1).wait_send()
 
-        @pl.loop(nl, nl + no)
-        def _(m):
-            in_remote(m).wait_recv()
+        @pl.loop(0, no)
+        def _(i):
+            in_remote(i).wait_recv()
 
     def sd(shape, dtype=BF16):
         return jax.ShapeDtypeStruct(shape, dtype)
 
     wl, dl = sd((nc, 2, dh, w)), sd((npr, fh, cw))
-    outs = (sd((rows, dh)), wl, sd((2, dh, fq)), wl, dl, sd((fh, dq)), dl, dl, dl)
+    outs = (pltpu.VMEM((rows, dh), BF16), wl, sd((2, dh, fq)), wl, dl, sd((fh, dq)), dl, dl, dl)
     dma = pltpu.SemaphoreType.DMA
     return pl.pallas_call(
         kernel,
         out_shape=outs,
         in_specs=[pl.BlockSpec(memory_space=pl.ANY)] * 4,
-        out_specs=[pl.BlockSpec(memory_space=pl.ANY)] * len(outs),
+        out_specs=[pl.BlockSpec(memory_space=pltpu.VMEM)] + [pl.BlockSpec(memory_space=pl.ANY)] * (len(outs) - 1),
         scratch_shapes=[
             pltpu.VMEM((rows, 2 * dh), BF16),
             pltpu.VMEM((rows, fh), BF16),
             pltpu.VMEM((ne, fh), BF16),
             pltpu.VMEM((2, 2 * dh, 2 * w), BF16),
             pltpu.VMEM((2, 2 * dh, 2 * w), BF16),
-            pltpu.VMEM((4, fh, cw), BF16),
+            pltpu.VMEM((2, fh, cw), BF16),
             pltpu.VMEM((lag + 1, tm, cw), F32),
             pltpu.VMEM((nk, tm, cw), F32),
             pltpu.VMEM((tm, cw), F32),
             pltpu.VMEM((oslots, tm, cw), BF16),
-            pltpu.VMEM((ne, cw), BF16),
             dma((2 * xc + 1,)), dma((2 * xc + 1,)),
             dma((nc, 2)), dma((nc, 2)), dma((nc, 2)), dma((nc, 2)), dma((nc, 2)), dma((nc, 2)), dma((3,)), dma((3,)),
             dma((npr,)), dma((npr,)), dma((npr,)), dma((npr,)), dma((npr,)), dma((npr,)), dma((npr,)), dma((npr,)),
-            dma((nk,)), dma((nk,)), dma((no,)), dma((no,)), dma((oslots + 1,)), dma((13,)),
+            dma((nk,)), dma((nk,)), dma((no,)), dma((no,)), dma((13,)),
         ],
         compiler_params=pltpu.CompilerParams(
-            collective_id=0, has_side_effects=True, vmem_limit_bytes=67043328),
-    )
-
-
-def copy_rows(shape):
-    n = 8
-    rows = shape[0] // n
-
-    def kernel(src, dst, buf, rs, ws):
-        part = [pl.ds(i * rows, rows) for i in range(n)]
-        reads = [pltpu.make_async_copy(src.at[p], buf.at[p], rs.at[i]) for i, p in enumerate(part)]
-        writes = [pltpu.make_async_copy(buf.at[p], dst.at[p], ws.at[i]) for i, p in enumerate(part)]
-        for r in reads:
-            r.start()
-        for r, c in zip(reads, writes):
-            r.wait()
-            c.start()
-        for c in writes:
-            c.wait()
-
-    return pl.pallas_call(
-        kernel,
-        out_shape=jax.ShapeDtypeStruct(shape, BF16),
-        in_specs=[pl.BlockSpec(memory_space=pl.ANY)],
-        out_specs=pl.BlockSpec(memory_space=pl.ANY),
-        scratch_shapes=[pltpu.VMEM(shape, BF16), pltpu.SemaphoreType.DMA((n,)), pltpu.SemaphoreType.DMA((n,))],
+            collective_id=0, has_side_effects=True, vmem_limit_bytes=67043328 - 2 * rows * dh),
     )
 
 
@@ -557,7 +512,6 @@
     w_out_spec = P("dz", ("dy", "dx"))
 
     def local_mlp(x_blk, wg_blk, wu_blk, wd_blk):
-        outs = make_local_mlp(x_blk.shape, wg_blk.shape, wd_blk.shape)(x_blk, wg_blk, wu_blk, wd_blk)
-        return copy_rows(x_blk.shape)(outs[0])
+        return make_local_mlp(x_blk.shape, wg_blk.shape, wd_blk.shape)(x_blk, wg_blk, wu_blk, wd_blk)[0]
 
     return jax.shard_map(local_mlp, mesh=mesh, in_specs=(x_spec, w_in_spec, w_in_spec, w_out_spec), out_specs=x_spec, check_vma=False)

time: 571 us -> 567 us (level)
  Pallas kernels: 569 us -> 563 us
where the time goes in v8:
time: 567 us; the launch traced here: 565 us
  Pallas kernels  563 us (99%)
    pallas_call x1, Pallas kernels, local_mlp(): make_local_mlp(x_blk.shape, wg_blk.shape, wd_blk.shape)  563 us

profile of v8, /device:TPU:0, one launch (start us, length us, event | category | flops | bytes accessed | tf_op | source)
XLA Modules:
  0.0 565.5 jit_solution(3354776016301886432)
XLA Ops:
  0.0 562.8 %shard_map.46 = (bf16[2048,1536]{1,0:T(8,128)(2,1)S(1)}, bf16[16,2,1536,128]{3,2,1,0:T(8,128)(2,1)}, bf16[2,1536,2048]{2,1,0:T(8,128)(2,1)}, bf16[16,2,1536,128]...) custom-call(bf16[2048,1536]{1,0:T(8,128)(2,1)} %x.1, ...), custom_call_target="tpu_custom_call" | custom-call | tf_op jit(solution)/shard_map/pallas_call | solution.py:515
  562.8 2.7 copy.6
